TPU v7x, 32 devices: a whole 2x2x4 slice. The times are simulated.
32 devices in a mesh: dp: 2 (over x), sp: 4 (over z), tp: 4 (over y, core).
Axes of the slice: x: 2, y: 2, z: 4, core: 2. Of those that a mesh axis runs over, the one named last changes fastest.
Arguments:
- hidden: bfloat16 [256, 4096], P('dp'), parts along dimension 0
- new_pos: int32 [256], P('dp'), parts along dimension 0
- k_self: bfloat16 [256, 256, 8, 128], P('dp', 'sp', 'tp'), parts along dimension 0
- v_self: bfloat16 [256, 256, 8, 128], P('dp', 'sp', 'tp'), parts along dimension 0
- k_cross: bfloat16 [256, 128, 8, 128], P('dp', None, 'tp'), parts along dimension 0
- v_cross: bfloat16 [256, 128, 8, 128], P('dp', None, 'tp'), parts along dimension 0
- xvalid: int32 [256, 128], P('dp'), parts along dimension 0
- rowmask: int32 [256], P('dp'), parts along dimension 0
- self_attn_norm: bfloat16 [4096], replicated
- self_wq: bfloat16 [4096, 4096], P(None, 'tp')
- self_wk: bfloat16 [4096, 1024], P(None, 'tp')
- self_wv: bfloat16 [4096, 1024], P(None, 'tp')
- self_wo: bfloat16 [4096, 4096], P('tp')
- self_mlp_norm: bfloat16 [4096], replicated
- self_wgate: bfloat16 [4096, 12288], P(None, 'tp')
- self_wup: bfloat16 [4096, 12288], P(None, 'tp')
- self_wdown: bfloat16 [12288, 4096], P('tp')
- cross_attn_norm: bfloat16 [4096], replicated
- cross_wq: bfloat16 [4096, 4096], P(None, 'tp')
- cross_qnorm: bfloat16 [128], replicated
- cross_wo: bfloat16 [4096, 4096], P('tp')
- cross_gates: float32 [2], replicated
- cross_mlp_norm: bfloat16 [4096], replicated
- cross_wgate: bfloat16 [4096, 12288], P(None, 'tp')
- cross_wup: bfloat16 [4096, 12288], P(None, 'tp')
- cross_wdown: bfloat16 [12288, 4096], P('tp')
Outputs:
- output 1: bfloat16 [256, 4096], P('dp'), parts along dimension 0
- output 2: bfloat16 [256, 256, 8, 128], P('dp', 'sp', 'tp'), parts along dimension 0
- output 3: bfloat16 [256, 256, 8, 128], P('dp', 'sp', 'tp'), parts along dimension 0
There are 2 independent parts. A program takes and returns all parts, laid end to end along the dimension named above; an argument that names none is the same for every part.
All inputs are finite; a program needn't handle non-finite values.
Results may differ from a plain program's by a relative error of at most 0.0149378.
Values sent between devices are 32-bit elements.
A program may use at most 1 GiB of HBM per device.

v0:
```python
import math
import jax
import jax.numpy as jnp
from jax import lax
from jax.sharding import PartitionSpec as P

NORM_EPS = 1e-5
ROPE_THETA = 500000.0
ROPE_FACTOR = 8.0
LOW_FREQ = 1.0
HIGH_FREQ = 4.0
ORIG_CTX = 8192.0
NEG_BIG = -1e30


def rope_freqs(head_dim):
    inv_freq = 1.0 / (ROPE_THETA ** (jnp.arange(0, head_dim, 2).astype(jnp.float32) / head_dim))
    wavelen = 2.0 * math.pi / inv_freq
    smooth = (ORIG_CTX / wavelen - LOW_FREQ) / (HIGH_FREQ - LOW_FREQ)
    mid_freq = (1.0 - smooth) * inv_freq / ROPE_FACTOR + smooth * inv_freq
    scaled = jnp.where(wavelen > ORIG_CTX / LOW_FREQ, inv_freq / ROPE_FACTOR, mid_freq)
    return jnp.where(wavelen < ORIG_CTX / HIGH_FREQ, inv_freq, scaled)


def apply_rope(vectors, positions):
    head_dim = vectors.shape[-1]
    half_dim = head_dim // 2
    angles = positions.astype(jnp.float32)[:, None] * rope_freqs(head_dim)[None, :]
    cos_t = jnp.cos(angles)[:, None, :]
    sin_t = jnp.sin(angles)[:, None, :]
    first_half = vectors[..., :half_dim]
    second_half = vectors[..., half_dim:]
    return jnp.concatenate([first_half * cos_t - second_half * sin_t, second_half * cos_t + first_half * sin_t], axis=-1)


def rms_norm(values, gain_vec):
    vals32 = values.astype(jnp.float32)
    inv_rms = lax.rsqrt(jnp.mean(vals32 * vals32, axis=-1, keepdims=True) + NORM_EPS)
    return (vals32 * inv_rms * gain_vec.astype(jnp.float32)).astype(jnp.bfloat16)


def mlp_partial(normed, w_gate, w_up, w_down):
    gate_val = jnp.dot(normed, w_gate, preferred_element_type=jnp.float32).astype(jnp.bfloat16)
    up_val = jnp.dot(normed, w_up, preferred_element_type=jnp.float32).astype(jnp.bfloat16)
    hidden_act = (jax.nn.silu(gate_val.astype(jnp.float32)) * up_val.astype(jnp.float32)).astype(jnp.bfloat16)
    return jnp.dot(hidden_act, w_down, preferred_element_type=jnp.float32)


def local_softmax(queries, key_rows, val_rows, valid_mask, score_scale):
    scores = jnp.einsum('bkgd,btkd->bkgt', queries, key_rows, preferred_element_type=jnp.float32) * score_scale
    scores = jnp.where(valid_mask, scores, NEG_BIG)
    part_max = jnp.max(scores, axis=-1)
    probs_loc = jnp.where(valid_mask, jnp.exp(scores - part_max[..., None]), 0.0)
    part_sum = jnp.sum(probs_loc, axis=-1)
    part_out = jnp.einsum('bkgt,btkd->bkgd', probs_loc.astype(jnp.bfloat16), val_rows, preferred_element_type=jnp.float32)
    return part_max, part_sum, part_out


def combine_sp(part_max, part_sum, part_out):
    glob_max = lax.pmax(part_max, 'sp')
    factor = jnp.exp(part_max - glob_max)
    total_sum = lax.psum(part_sum * factor, 'sp')
    total_out = lax.psum(part_out * factor[..., None], 'sp')
    return total_out / total_sum[..., None]


def solution(mesh):
    cache_spec = P('dp', 'sp', 'tp', None)
    cross_spec = P('dp', None, 'tp', None)
    row_spec = P('dp', None)
    vec_spec = P('dp')
    full_spec = P(None)
    col_spec = P(None, 'tp')
    split_rows = P('tp', None)
    in_specs = (row_spec, vec_spec, cache_spec, cache_spec, cross_spec, cross_spec, row_spec, vec_spec,
                full_spec, col_spec, col_spec, col_spec, split_rows, full_spec, col_spec, col_spec, split_rows,
                full_spec, col_spec, full_spec, split_rows, full_spec, full_spec, col_spec, col_spec, split_rows)
    out_specs = (row_spec, cache_spec, cache_spec)

    def local_step(hidden, new_pos, k_self, v_self, k_cross, v_cross, xvalid, rowmask,
                   self_attn_norm, self_wq, self_wk, self_wv, self_wo, self_mlp_norm,
                   self_wgate, self_wup, self_wdown, cross_attn_norm, cross_wq, cross_qnorm,
                   cross_wo, cross_gates, cross_mlp_norm, cross_wgate, cross_wup, cross_wdown):
        batch_rows = hidden.shape[0]
        len_local = k_self.shape[1]
        kv_local = k_self.shape[2]
        head_dim = k_self.shape[3]
        heads_local = self_wq.shape[1] // head_dim
        group_size = heads_local // kv_local
        score_scale = head_dim ** -0.5
        normed = rms_norm(hidden, self_attn_norm)
        queries = jnp.dot(normed, self_wq, preferred_element_type=jnp.float32).astype(jnp.bfloat16)
        key_new = jnp.dot(normed, self_wk, preferred_element_type=jnp.float32).astype(jnp.bfloat16)
        val_new = jnp.dot(normed, self_wv, preferred_element_type=jnp.float32).astype(jnp.bfloat16)
        queries = apply_rope(queries.reshape(batch_rows, heads_local, head_dim).astype(jnp.float32), new_pos).astype(jnp.bfloat16)
        key_new = apply_rope(key_new.reshape(batch_rows, kv_local, head_dim).astype(jnp.float32), new_pos).astype(jnp.bfloat16)
        val_new = val_new.reshape(batch_rows, kv_local, head_dim)
        local_pos = new_pos - lax.axis_index('sp') * len_local
        slot_ids = jnp.arange(len_local)
        hit_mask = (slot_ids[None, :] == local_pos[:, None])[:, :, None, None]
        k_new_cache = jnp.where(hit_mask, key_new[:, None], k_self)
        v_new_cache = jnp.where(hit_mask, val_new[:, None], v_self)
        seen_mask = (slot_ids[None, :] <= local_pos[:, None])[:, None, None, :]
        self_stats = local_softmax(queries.reshape(batch_rows, kv_local, group_size, head_dim), k_new_cache, v_new_cache, seen_mask, score_scale)
        self_attn = combine_sp(self_stats[0], self_stats[1], self_stats[2])
        self_flat = self_attn.astype(jnp.bfloat16).reshape(batch_rows, heads_local * head_dim)
        attn_sum = lax.psum(jnp.dot(self_flat, self_wo, preferred_element_type=jnp.float32), 'tp')
        after_attn = (hidden.astype(jnp.float32) + attn_sum).astype(jnp.bfloat16)
        mlp_sum = lax.psum(mlp_partial(rms_norm(after_attn, self_mlp_norm), self_wgate, self_wup, self_wdown), 'tp')
        after_mlp = (after_attn.astype(jnp.float32) + mlp_sum).astype(jnp.bfloat16)
        normed = rms_norm(after_mlp, cross_attn_norm)
        cross_q = jnp.dot(normed, cross_wq, preferred_element_type=jnp.float32).astype(jnp.bfloat16)
        cross_q = rms_norm(cross_q.reshape(batch_rows, heads_local, head_dim), cross_qnorm)
        cross_mask = (xvalid > 0)[:, None, None, :]
        cross_stats = local_softmax(cross_q.reshape(batch_rows, kv_local, group_size, head_dim), k_cross, v_cross, cross_mask, score_scale)
        cross_attn = cross_stats[2] / cross_stats[1][..., None]
        cross_flat = cross_attn.astype(jnp.bfloat16).reshape(batch_rows, heads_local * head_dim)
        gate_vals = jnp.tanh(cross_gates.astype(jnp.float32))
        row_scale = rowmask.astype(jnp.float32)[:, None]
        xattn_sum = lax.psum(jnp.dot(cross_flat, cross_wo, preferred_element_type=jnp.float32), 'tp')
        after_cross = (after_mlp.astype(jnp.float32) + gate_vals[0] * row_scale * xattn_sum).astype(jnp.bfloat16)
        xmlp_sum = lax.psum(mlp_partial(rms_norm(after_cross, cross_mlp_norm), cross_wgate, cross_wup, cross_wdown), 'tp')
        after_xmlp = (after_cross.astype(jnp.float32) + gate_vals[1] * row_scale * xmlp_sum).astype(jnp.bfloat16)
        return after_xmlp, k_new_cache, v_new_cache

    return jax.shard_map(local_step, mesh=mesh, in_specs=in_specs, out_specs=out_specs, check_vma=False)
```

profile of v0, /device:TPU:0, one launch (start us, length us, event | category | flops | bytes accessed | tf_op | source)
XLA Modules:
  0.0 419.5 jit_solution(15411880043427541267)
XLA Ops:
  7.2 0.0 copy-start
  7.2 0.0 all-reduce.6.cloned.1.call-start
  7.3 0.8 convert_element_type.158
  8.1 1.5 fusion.19
  9.6 1.8 fusion.63
  11.4 0.0 copy-start.11
  11.4 0.1 reshape.217
  11.5 2.1 convolution_convert_fusion.6
  13.7 0.1 iota_compare_fusion.1
  13.8 0.0 copy-start.3
  13.8 0.0 copy-start.4
  13.8 4.8 %fusion.59 = f32[16,8,8,128]{3,1,2,0:T(8,128)S(1)} fusion(bf16[4096,1024]{1,0:T(8,128)(2,1)} %param.35, bf16[128,4096]{1,0:T(8,128)(2,1)S(1)} %copy-done.2, f32[4096]{0:T(1024)S(1)} %convert_element_type.158, f32[128]{0:T(128)S(1)} %add_rsqrt_fusion.4), kind=kOutput, calls=%fused_computation.73 | convolution fusion | flops 1076101120 | bytes 9978368 | tf_op jit(solution)/shard_map/dot_general | solution.py:92
  18.6 0.1 copy.50
  18.7 0.3 multiply_cosine_fusion
  19.0 0.3 subtract_convert_fusion.1
  19.3 0.3 subtract_convert_fusion
  19.6 0.2 pad_maximum_fusion
  19.8 12.7 %broadcast_select_fusion.1 = (bf16[128,64,2,128]{3,2,1,0:T(2,128)(2,1)S(1)}, bf16[128,64,2,128]{3,2,1,0:T(2,128)(2,1)}) fusion(bf16[128,64,2,128]{3,2,1,0:T(2,128)(2,1)S(1)} %copy-done.3, pred[128,64]{1,0:T(8,128)(4,1)S(1)} %get-tuple-element.24, bf16[128,2,128]{2,1,0:T(2,128)(2,1)S(1)} %pad_maximum_fusion, bf16[128,64,2,128]{3,2,1,0:T(2,128)(2,1)S(1)} %copy-done.4, ...), kind=kLoop, calls=%fused_computation.6 | loop fusion | flops 4194304 | bytes 16916480 | tf_op jit(solution)/shard_map/jit(_where)/select_n | solution.py:101
  32.5 2.7 fusion.109
  35.2 22.9 %pmax.7 = f32[128,2,4]{2,1,0:T(2,128)S(1)} all-reduce(f32[128,2,4]{2,1,0:T(2,128)S(1)} %get-tuple-element.27), channel_id=1, replica_groups=mesh['dp'=2,'sp'=4,'tp'=4] {'sp'}, use_global_device_ids=true, to_apply=%region_2.3 | all-reduce | flops 1024 | bytes 8192 | tf_op jit(solution)/shard_map/pmax | solution.py:60
  58.1 0.8 fusion.78
  59.0 4.3 %fusion.51 = f32[128,2,4,128]{3,2,1,0:T(4,128)} fusion(bf16[128,64,2,128]{3,2,1,0:T(2,128)(2,1)} %get-tuple-element.16, f32[128,2,4,64]{3,2,1,0:T(4,128)S(1)} %get-tuple-element.28, f32[128,2,4]{2,1,0:T(2,128)S(1)} %bitcast.39, f32[128,2,4]{2,1,0:T(2,128)S(1)} %get-tuple-element.27, pred[128,64]{1,0:T(8,128)(4,1)S(1)} %get-tuple-element.23), kind=kOutput, calls=%fused_computation.67 | convolution fusion | flops 17104896 | bytes 4997120 | tf_op jit(solution)/shard_map/bkgt,btkd->bkgd/dot_general | solution.py:55
  63.2 0.0 all-reduce.6.cloned.1.call-update
  63.2 0.0 all-reduce.8.cloned.1.call-start
  63.3 19.5 %psum.43 = f32[128,2,4]{2,1,0:T(2,128)S(1)} all-reduce(f32[128,2,4]{2,1,0:T(2,128)S(1)} %bitcast.35), channel_id=1, replica_groups=mesh['dp'=2,'sp'=4,'tp'=4] {'sp'}, use_global_device_ids=true, to_apply=%region_5.6 | all-reduce | flops 1024 | bytes 8192 | tf_op jit(solution)/shard_map/psum | solution.py:62
  82.8 18.4 %all-reduce.6.cloned.1.call-done = f32[128,2,4,128]{3,2,1,0:T(4,128)} async-done(((f32[128,2,4,128]{3,2,1,0:T(4,128)}), f32[128,2,4,128]{3,2,1,0:T(4,128)}) %all-reduce.6.cloned.1.call-update) | async-done | bytes 524304 | tf_op jit(solution)/shard_map/psum | solution.py:63
  101.2 1.4 divide_convert_fusion
  102.6 0.2 reshape.214
  102.8 5.9 %fusion.113 = f32[128,4096]{1,0:T(8,128)} fusion(bf16[128,1024]{1,0:T(8,128)(2,1)S(1)} %reshape.214, bf16[1024,4096]{1,0:T(8,128)(2,1)} %param.38), kind=kOutput, calls=%fused_computation.130 | convolution fusion | flops 1073741824 | bytes 10747904 | tf_op jit(solution)/shard_map/dot_general | solution.py:107
  108.7 0.0 all-reduce.8.cloned.1.call-update
  108.7 0.2 all-reduce.10.cloned.1.call-start
  109.0 0.4 copy-done.7
  109.4 50.4 %all-reduce.8.cloned.1.call-done = f32[128,4096]{1,0:T(8,128)} async-done(((f32[128,4096]{1,0:T(8,128)}), f32[128,4096]{1,0:T(8,128)}) %all-reduce.8.cloned.1.call-update) | async-done | bytes 2097168 | tf_op jit(solution)/shard_map/psum | solution.py:107
  159.8 2.0 fusion.23
  161.8 12.8 %fusion.16 = f32[128,3072]{1,0:T(8,128)} fusion(bf16[4096,3072]{1,0:T(8,128)(2,1)} %param.40, bf16[128,4096]{1,0:T(8,128)(2,1)S(1)} %get-tuple-element.8, f32[4096]{0:T(1024)S(1)} %convert_element_type.173, f32[128]{0:T(128)S(1)} %add_rsqrt_fusion.3), kind=kOutput, calls=%fused_computation.22 | convolution fusion | flops 3224109056 | bytes 27804160 | tf_op jit(solution)/shard_map/dot_general | solution.py:43
  174.6 20.9 %fusion.17 = f32[128,4096]{1,0:T(8,128)} fusion(bf16[3072,4096]{1,0:T(8,128)(2,1)} %param.42, bf16[4096,3072]{1,0:T(8,128)(2,1)} %param.41, f32[128,3072]{1,0:T(8,128)} %fusion.16, bf16[128,4096]{1,0:T(8,128)(2,1)S(1)} %get-tuple-element.8, f32[4096]{0:T(1024)S(1)} %convert_element_type.173, f32[128]{0:T(128)S(1)} %add_rsqrt_fusion.3), kind=kOutput, calls=%fused_computation.23 | convolution fusion | flops 6447693824 | bytes 55067136 | tf_op jit(solution)/shard_map/dot_general | solution.py:46
  195.5 0.0 all-reduce.10.cloned.1.call-update
  195.6 0.3 all-reduce.12.cloned.1.call-start
  195.8 0.4 copy-done.8
  196.2 0.2 copy-done.6
  196.4 50.6 %all-reduce.10.cloned.1.call-done = f32[128,4096]{1,0:T(8,128)} async-done(((f32[128,4096]{1,0:T(8,128)}), f32[128,4096]{1,0:T(8,128)}) %all-reduce.10.cloned.1.call-update) | async-done | bytes 2097168 | tf_op jit(solution)/shard_map/psum | solution.py:109
  247.0 2.0 fusion.27
  249.0 4.7 %fusion.57 = f32[128,1024]{1,0:T(8,128)S(1)} fusion(bf16[4096,1024]{1,0:T(8,128)(2,1)} %param.44, bf16[128,4096]{1,0:T(8,128)(2,1)S(1)} %get-tuple-element.6, f32[4096]{0:T(1024)S(1)} %convert_element_type.183, f32[128]{0:T(128)S(1)} %add_rsqrt_fusion.2), kind=kOutput, calls=%fused_computation.70 | convolution fusion | flops 1076101120 | bytes 9978368 | tf_op jit(solution)/shard_map/dot_general | solution.py:112
  253.7 0.2 reshape.218
  254.0 0.1 copy.51
  254.1 0.2 reduce_sum.67
  254.4 0.2 copy.47
  254.5 8.1 %fusion.110 = (f32[128,2,4]{2,1,0:T(2,128)S(1)}, bf16[128,2,4,128]{3,2,1,0:T(4,128)(2,1)S(1)}) fusion(pred[128,128]{1,0:T(8,128)(4,1)S(1)} %broadcast_compare_fusion, bf16[128,128,2,128]{3,2,1,0:T(2,128)(2,1)} %param.30, f32[128,2,4,128]{3,2,1,0:T(4,128)S(1)} %reshape.218, f32[128]{0:T(128)S(1)} %convert_element_type.189, f32[128,2,4]{2,1,0:T(2,128)S(1)} %copy.47), kind=kOutput, calls=%fused_computation.129 | convolution fusion | flops 34734208 | bytes 9200128 | tf_op jit(solution)/shard_map/sub | solution.py:53
  262.7 5.7 %fusion.73 = bf16[128,2,4,128]{3,2,1,0:T(4,128)(2,1)S(1)} fusion(bf16[128,128,2,128]{3,2,1,0:T(2,128)(2,1)} %param.31, f32[128,2,4]{2,1,0:T(2,128)S(1)} %get-tuple-element.29, bf16[128,2,4,128]{3,2,1,0:T(4,128)(2,1)S(1)} %get-tuple-element.30), kind=kOutput, calls=%fused_computation.82 | convolution fusion | flops 33816576 | bytes 8916992 | tf_op jit(solution)/shard_map/bkgt,btkd->bkgd/dot_general | solution.py:55
  268.3 0.2 reshape.215
  268.5 5.9 %fusion.114 = f32[128,4096]{1,0:T(8,128)} fusion(bf16[128,1024]{1,0:T(8,128)(2,1)S(1)} %reshape.215, bf16[1024,4096]{1,0:T(8,128)(2,1)} %param.46), kind=kOutput, calls=%fused_computation.131 | convolution fusion | flops 1073741824 | bytes 10747904 | tf_op jit(solution)/shard_map/dot_general | solution.py:120
  274.5 0.0 all-reduce.12.cloned.1.call-update
  274.5 0.3 all-reduce.14.cloned.1.call-start
  274.8 0.3 copy-done.13
  275.1 0.1 copy-done.9
  275.2 0.6 fusion.107
  275.8 1.3 convert_multiply_fusion.8
  277.0 48.9 %all-reduce.12.cloned.1.call-done = f32[128,4096]{1,0:T(8,128)} async-done(((f32[128,4096]{1,0:T(8,128)}), f32[128,4096]{1,0:T(8,128)}) %all-reduce.12.cloned.1.call-update) | async-done | bytes 2097168 | tf_op jit(solution)/shard_map/psum | solution.py:120
  325.9 2.2 fusion.31
  328.1 10.0 %fusion.12 = f32[128,3072]{1,0:T(8,128)S(1)} fusion(bf16[4096,3072]{1,0:T(8,128)(2,1)} %param.49, bf16[128,4096]{1,0:T(8,128)(2,1)S(1)} %get-tuple-element.4, f32[4096]{0:T(1024)S(1)} %convert_element_type.195, f32[128]{0:T(128)S(1)} %add_rsqrt_fusion.1), kind=kOutput, calls=%fused_computation.16 | convolution fusion | flops 3224109056 | bytes 27804160 | tf_op jit(solution)/shard_map/dot_general | solution.py:43
  338.1 20.3 %fusion.18 = f32[128,4096]{1,0:T(8,128)} fusion(bf16[3072,4096]{1,0:T(8,128)(2,1)} %param.51, bf16[4096,3072]{1,0:T(8,128)(2,1)} %param.50, f32[128,3072]{1,0:T(8,128)S(1)} %fusion.12, bf16[128,4096]{1,0:T(8,128)(2,1)S(1)} %get-tuple-element.4, f32[4096]{0:T(1024)S(1)} %convert_element_type.195, f32[128]{0:T(128)S(1)} %add_rsqrt_fusion.1), kind=kOutput, calls=%fused_computation.24 | convolution fusion | flops 6447693824 | bytes 55067136 | tf_op jit(solution)/shard_map/dot_general | solution.py:46
  358.4 0.0 all-reduce.14.cloned.1.call-update
  358.5 51.4 %all-reduce.14.cloned.1.call-done = f32[128,4096]{1,0:T(8,128)} async-done(((f32[128,4096]{1,0:T(8,128)}), f32[128,4096]{1,0:T(8,128)}) %all-reduce.14.cloned.1.call-update) | async-done | bytes 2097168 | tf_op jit(solution)/shard_map/psum | solution.py:122
  409.9 3.0 fusion.34
  (36 shorter events, 0.3 us)
Async XLA Ops:
  7.2 2.5 copy-start
  7.2 94.0 %all-reduce.6.cloned.1.call-start = ((), (), s32[]{:S(2)}) async-start(), calls=%async_computation | async-start | bytes 1048576 | tf_op jit(solution)/shard_map/psum | solution.py:63
  9.6 1.9 copy-start.2
  11.4 2.2 copy-start.11
  13.8 6.0 %copy-start.3 = (bf16[128,64,2,128]{3,2,1,0:T(2,128)(2,1)S(1)}, bf16[128,64,2,128]{3,2,1,0:T(2,128)(2,1)}, u32[]{:S(2)}) copy-start(bf16[128,64,2,128]{3,2,1,0:T(2,128)(2,1)} %param.28) | copy-start | bytes 12582916
  13.8 6.0 %copy-start.4 = (bf16[128,64,2,128]{3,2,1,0:T(2,128)(2,1)S(1)}, bf16[128,64,2,128]{3,2,1,0:T(2,128)(2,1)}, u32[]{:S(2)}) copy-start(bf16[128,64,2,128]{3,2,1,0:T(2,128)(2,1)} %param.29) | copy-start | bytes 12582916
  32.5 2.7 copy-start.5
  63.2 96.6 %all-reduce.8.cloned.1.call-start = ((), (), s32[]{:S(2)}) async-start(), calls=%async_computation.1 | async-start | bytes 4194304 | tf_op jit(solution)/shard_map/psum | solution.py:107
  108.7 0.7 copy-start.7
  108.7 138.2 %all-reduce.10.cloned.1.call-start = ((), (), s32[]{:S(2)}) async-start(), calls=%async_computation.2 | async-start | bytes 4194304 | tf_op jit(solution)/shard_map/psum | solution.py:109
  195.5 0.7 copy-start.8
  195.5 0.7 copy-start.12
  195.5 0.9 copy-start.6
  195.6 130.4 %all-reduce.12.cloned.1.call-start = ((), (), s32[]{:S(2)}) async-start(), calls=%async_computation.3 | async-start | bytes 4194304 | tf_op jit(solution)/shard_map/psum | solution.py:120
  274.4 0.7 copy-start.13
  274.4 0.7 copy-start.9
  274.5 1.3 copy-start.10
  274.5 135.4 %all-reduce.14.cloned.1.call-start = ((), (), s32[]{:S(2)}) async-start(), calls=%async_computation.4 | async-start | bytes 4194304 | tf_op jit(solution)/shard_map/psum | solution.py:122
  409.9 3.0 copy-start.1
Sparse Core Ops, SparseCore 0:
  63.4 37.7 all-reduce.5
  108.9 50.9 all-reduce.7
  195.7 51.2 all-reduce.9
  274.6 51.2 all-reduce.11
  358.6 51.2 all-reduce.13
where the time goes:
time: 420 us; the launch traced here: 419 us
  waiting for transfers between devices  220 us (52%)
  matrix products  110 us (26%)
  blocking collectives  42.4 us (10%)
  other arithmetic  29.1 us (7%)
  between operations  14.1 us (3%)
    psum x1, waiting for transfers between devices, local_step(): lax.psum(mlp_partial(rms_norm(after_cross, cross_mlp_norm), cross_wgate,...  51.4 us
    psum x1, waiting for transfers between devices, local_step(): lax.psum(mlp_partial(rms_norm(after_attn, self_mlp_norm), self_wgate, sel...  50.6 us
    psum x1, waiting for transfers between devices, local_step(): lax.psum(jnp.dot(self_flat, self_wo, preferred_element_type=jnp.float32),...  50.4 us
    psum x1, waiting for transfers between devices, local_step(): lax.psum(jnp.dot(cross_flat, cross_wo, preferred_element_type=jnp.float32...  48.9 us
    dot_general x2, matrix products, mlp_partial(): return jnp.dot(hidden_act, w_down, preferred_element_type=jnp.float32)  41.2 us
    pmax x1, blocking collectives, combine_sp(): glob_max = lax.pmax(part_max, 'sp')  22.9 us
    dot_general x2, matrix products, mlp_partial(): jnp.dot(normed, w_gate, preferred_element_type=jnp.float32)  22.8 us
    psum x1, blocking collectives, combine_sp(): total_sum = lax.psum(part_sum * factor, 'sp')  19.5 us
  transfers between devices with their start and end apart: 5, of which 5 were waited for; matrix products, arithmetic and copies ran while one was open for 0% of the time, Pallas kernels for 0%

commit v1 on v0

v1 whole, which is shorter than its diff:
```python
import math
import jax
import jax.numpy as jnp
from jax import lax
from jax.experimental import pallas as pl
from jax.experimental.pallas import tpu as pltpu
from jax.sharding import PartitionSpec as P

NORM_EPS = 1e-5
ROPE_THETA = 500000.0
ROPE_FACTOR = 8.0
LOW_FREQ = 1.0
HIGH_FREQ = 4.0
ORIG_CTX = 8192.0
NEG_BIG = -1e30
F32 = jnp.float32
BF16 = jnp.bfloat16
I32 = jnp.int32
MESH = pl.DeviceIdType.MESH
ANY = pl.ANY
VMEM = pltpu.VMEM
SMEM = pltpu.SMEM
NS = 23
B = 128
R = 32
HR = 16
W = 4096
D = 128
HL = 8
QW = 1024
FF = 3072
SPAN = 64
NG = 4
HC = 512
QC = 256
SCALE = D ** -0.5
MAXV = 67043328
NT = (((1,), (1,)), ((), ()))
WIN = {'preferred_element_type': F32}
ORDER = (2, 1, 3, 0)


def iota(shape, axis):
    return lax.broadcasted_iota(I32, shape, axis)


def rotary_freqs(lane):
    inv = jnp.exp((lane % SPAN).astype(F32) * (-2.0 / D * math.log(ROPE_THETA)))
    wave = 2.0 * math.pi / inv
    smooth = (ORIG_CTX / wave - LOW_FREQ) / (HIGH_FREQ - LOW_FREQ)
    mid = (1.0 - smooth) * inv / ROPE_FACTOR + smooth * inv
    scaled = jnp.where(wave > ORIG_CTX / LOW_FREQ, inv / ROPE_FACTOR, mid)
    return jnp.where(wave < ORIG_CTX / HIGH_FREQ, inv, scaled)


def norm_rows(src, gain, dst, r0, rows):
    at = slice(r0, r0 + rows)
    total = jnp.zeros((rows, D), F32)
    for c in range(0, W, D):
        v = src[at, c:c + D].astype(F32)
        total = total + v * v
    inv = lax.rsqrt(jnp.sum(total, axis=-1, keepdims=True) / W + NORM_EPS)
    for c in range(0, W, D):
        g = gain[c // D:c // D + 1, :].astype(F32)
        dst[at, c:c + D] = (src[at, c:c + D].astype(F32) * inv * g).astype(BF16)


def big_dot(lhs, rhs_of, depth, step=1024):
    acc = None
    for k in range(0, depth, step):
        part = jnp.dot(lhs[:, k:k + step], rhs_of(k, step), **WIN)
        acc = part if acc is None else acc + part
    return acc


def self_kernel(pos_s, g1, pos_a, hid, wq, wk, wv, kc, vc, kout, vout, qout,
                hb, xb, wb, kb, vb, q3, kn, vn, cs, sn, pv, w_sem, c_sem, o_sem, p_sem):
    base = lax.axis_index('sp') * SPAN

    def wcopy(i):
        src = (wk, wv)[i] if i < 2 else wq.at[:, (i - 2) * QC:(i - 1) * QC]
        return pltpu.make_async_copy(src, wb.at[i], w_sem.at[i])

    def ccopy(j):
        r = pl.ds((j // 2) * R, R)
        src, dst = ((kc, kb), (vc, vb))[j % 2]
        return pltpu.make_async_copy(src.at[r], dst.at[r], c_sem.at[j])

    def ocopy(j):
        r = pl.ds((j // 2) * R, R)
        src, dst = ((kb, kout), (vb, vout))[j % 2]
        return pltpu.make_async_copy(src.at[r], dst.at[r], o_sem.at[j])

    pcopy = pltpu.make_async_copy(pos_a, pv, p_sem.at[0])
    hcopy = pltpu.make_async_copy(hid, hb, p_sem.at[1])
    qcopy = pltpu.make_async_copy(q3, qout, p_sem.at[2])
    pcopy.start()
    hcopy.start()
    for i in range(2):
        wcopy(i).start()
    for j in range(2 * NG):
        ccopy(j).start()
    for i in range(2, 6):
        wcopy(i).start()

    pcopy.wait()
    ri = iota((B, D), 0)
    ci = iota((B, D), 1)
    posf = jnp.broadcast_to(pv[...].astype(F32), (B, D))
    pos_col = jnp.sum(jnp.where(ri == ci, posf, 0.0), axis=1, keepdims=True)
    ang = pos_col * jnp.broadcast_to(rotary_freqs(iota((1, D), 1)), (B, D))
    cs[...] = jnp.cos(ang)
    sn[...] = jnp.sin(ang) * jnp.where(ci < SPAN, -1.0, 1.0)

    hcopy.wait()
    norm_rows(hb, g1, xb, 0, B)

    def project(i):
        wcopy(i).wait()
        y = big_dot(xb, lambda k, w: wb[i, k:k + w, :], W).astype(BF16).astype(F32)
        for h in range(2):
            t = y[:, h * D:(h + 1) * D]
            if i != 1:
                t = t * cs[...] + pltpu.roll(t, SPAN, 1) * sn[...]
            t = t.astype(BF16).astype(F32)
            if i > 1:
                q3[:, (i - 2) * 2 + h, :] = t
            else:
                (kn, vn)[i][h] = t

    project(0)
    project(1)
    row16 = iota((HR, D), 0)
    for j in range(NG):
        ccopy(2 * j).wait()
        ccopy(2 * j + 1).wait()

        def body(it, _):
            for u in range(HL):
                b = j * R + it * HL + u
                lp = pos_s[b] - base
                t0 = pl.multiple_of((jnp.clip(lp, 0, SPAN - 1) // HL) * HR, HR)
                hit = row16 + t0 - 2 * lp
                for buf, new in ((kb, kn), (vb, vn)):
                    old = buf[b, pl.ds(t0, HR), :].astype(F32)
                    upd = jnp.where(hit == 0, new[0, pl.ds(b, 1), :], jnp.where(hit == 1, new[1, pl.ds(b, 1), :], old))
                    buf[b, pl.ds(t0, HR), :] = upd.astype(BF16)
            return 0
        lax.fori_loop(0, R // HL, body, 0)
        ocopy(2 * j).start()
        ocopy(2 * j + 1).start()
    for i in range(2, 6):
        project(i)
    qcopy.start()
    for j in range(2 * NG):
        ocopy(j).wait()
    qcopy.wait()


def rest_kernel(pos_s, mask_s, gates, g2, g3, g4, qn, q_in, ks, vs, hid, xval, kc, vc,
                wo, wg1, wu1, wd1, wqc, woc, wg2, wu2, wd2, out,
                slots, qb, ob, orecv, hrow, h, x, act, o2, q3, kb, vb, xv, xl,
                p0, m0, s1, t1, rb1, rb2, rb3, rbq, fin,
                w_sem, m_sem, k_sem, sp_send, sp_recv, a_send, a_recv, y_send, y_recv,
                b_send, b_recv, z_send, z_recv, f_send, f_recv, e_send, e_recv):
    sp = lax.axis_index('sp')
    tp = lax.axis_index('tp')
    core = tp % 2
    ypos = tp // 2
    sib = {'tp': tp + 1 - 2 * core}
    ypeer = {'tp': (tp + 2) % 4}
    row0 = pl.multiple_of(sp * R, R)
    other = 1 - core

    def half_col(g, half):
        return pl.multiple_of(g * 1024 + half * HC, HC)

    def remote(src, dst, ssem, rsem, dev):
        return pltpu.make_async_remote_copy(src, dst, ssem, rsem, device_id=dev, device_id_type=MESH)

    def cols(ref, c):
        return ref.at[:, pl.ds(pl.multiple_of(c, QC), QC)]

    def start(src, dst, slot):
        pltpu.make_async_copy(src, dst, w_sem.at[slot]).start()

    def put_o(ref):
        def f(j, slot):
            for k in range(4):
                half = other if k < 2 else core
                start(cols(ref, half_col(j, half) + (k % 2) * QC), slots.at[slot, k * QW:(k + 1) * QW], slot)
        return f

    def put_gu(gate, up):
        def f(j, slot):
            for n, ref in enumerate((gate, up)):
                @pl.when(j % 2 == n)
                def _():
                    start(cols(ref, (j // 2) * QC), slots.at[slot], slot)
        return f

    def put_down(ref):
        def f(j, slot):
            k = j % 4
            half = jnp.where(k < 2, other, core)
            start(cols(ref, half_col(j // 4, half) + (k % 2) * QC), slots.at[slot, 0:FF], slot)
        return f

    def put_q(ref):
        def f(j, slot):
            start(cols(ref, j * QC), slots.at[slot], slot)
        return f

    segs = []
    pos = 0
    for count, f in ((4, put_o(wo)), (24, put_gu(wg1, wu1)), (16, put_down(wd1)), (4, put_q(wqc)),
                     (4, put_o(woc)), (24, put_gu(wg2, wu2)), (16, put_down(wd2))):
        segs.append((pos, pos + count, f))
        pos += count

    def issue(i, lo, hi):
        for a, b, f in segs:
            if a <= lo and b >= hi:
                f(i - a, lax.rem(i, NS))
            elif a < hi and b > lo:
                @pl.when((i >= a) & (i < b))
                def _():
                    f(i - a, lax.rem(i, NS))

    def wait_item(i, depth=W):
        slot = lax.rem(i, NS)
        pltpu.make_async_copy(cols(wqc, 0).at[0:depth], slots.at[slot, 0:depth], w_sem.at[slot]).wait()
        return slot

    def refill(i, lo, hi):
        issue(i + NS, lo + NS, hi + NS)

    def dest_of(n):
        return (sp + ORDER[n % NG]) % NG

    def kv_self(n):
        r = pl.ds(pl.multiple_of(dest_of(n) * R + (n // NG) * HR, HR), HR)
        return [pltpu.make_async_copy(src.at[r], dst.at[n % NG], k_sem.at[i, n % NG])
                for i, (src, dst) in enumerate(((ks, kb), (vs, vb)))]

    def kv_cross(n):
        r = pl.ds(pl.multiple_of(row0 + (n // 2) * HR, HR), HR)
        return [pltpu.make_async_copy(src.at[r, n % 2], dst.at[n], k_sem.at[i, n])
                for i, (src, dst) in enumerate(((kc, kb), (vc, vb)))]

    def go(cs):
        for c in cs:
            c.start()

    def fin_wait(cs):
        for c in cs:
            c.wait()

    qcopy = pltpu.make_async_copy(q_in, qb, m_sem.at[0])
    hcopy = pltpu.make_async_copy(hid.at[pl.ds(row0, R)], hrow, m_sem.at[1])
    xcopy = pltpu.make_async_copy(xval.at[pl.ds(row0, R)], xv, m_sem.at[2])
    go([qcopy])
    for n in range(NG):
        go(kv_self(n))
    go([hcopy, xcopy])

    def fill(i, _):
        issue(i, 0, NS)
        return 0
    lax.fori_loop(0, NS, fill, 0)

    barrier = pltpu.get_barrier_semaphore()
    for dev in [{'sp': (sp + d) % NG} for d in ORDER[:3]] + [sib, ypeer]:
        pl.semaphore_signal(barrier, inc=1, device_id=dev, device_id_type=MESH)
    pl.semaphore_wait(barrier, 5)

    lane = iota((HL, D), 1)
    par = (lane % 2) == (iota((HL, D), 0) // 4)

    def scores(q, k):
        return lax.dot_general(q.astype(BF16), k, NT, **WIN) * SCALE

    def sp_copy(n):
        d = ORDER[n % NG]
        half = n // NG
        return remote(ob.at[d, half], orecv.at[sp, half], sp_send.at[half, d], sp_recv.at[half, d],
                      {'sp': dest_of(n)})

    def attend_stage(n):
        half = n // NG
        d = ORDER[n % NG]
        fin_wait(kv_self(n))
        first = dest_of(n) * R + half * HR
        slot = n % NG

        def body(it, st):
            res = []
            for u in range(HL):
                v = it * HL + u
                lp = pos_s[first + v] - sp * SPAN
                s = scores(qb[first + v], kb[slot, v])
                ok = par & (lane <= 2 * lp + 1)
                s = jnp.where(ok, s, NEG_BIG)
                m = jnp.max(s, axis=-1, keepdims=True)
                p = jnp.where(ok, jnp.exp(s - m), 0.0)
                res.append((m, jnp.sum(p, axis=-1, keepdims=True), p))
            for u in range(HL):
                v = it * HL + u
                m, l, p = res[u]
                o = jnp.dot(p.astype(BF16), vb[slot, v], **WIN)
                if d:
                    ob[d, half, v] = o
                else:
                    orecv[sp, half, v] = o
                st = jnp.where(lane == v, m, jnp.where(lane == HR + v, l, st))
            return st
        st = lax.fori_loop(0, HR // HL, body, jnp.zeros((HL, D), F32))
        if d:
            ob[d, half, HR] = st
            sp_copy(n).start()
        else:
            orecv[sp, half, HR] = st

    def combine(half):
        for n in range(NG * half, NG * half + 3):
            sp_copy(n).wait_recv()
        st = [orecv[s, half, HR] for s in range(NG)]
        gm = jnp.maximum(jnp.maximum(st[0], st[1]), jnp.maximum(st[2], st[3]))
        fac = [jnp.exp(v - gm) for v in st]
        tot = jnp.zeros((HL, D), F32)
        for v, f in zip(st, fac):
            tot = tot + pltpu.roll(v, D - HR, 1) * f
        wts = [f / tot for f in fac]
        for r in range(HR):
            acc = jnp.zeros((HL, D), F32)
            for s in range(NG):
                acc = acc + orecv[s, half, r] * wts[s][:, r:r + 1]
            q3[half * HR + r] = acc
        flatten(half)

    def flatten(half):
        at = slice(half * HR, half * HR + HR)
        for hh in range(HL):
            o2[at, hh * D:(hh + 1) * D] = q3[at, hh, :].astype(BF16)

    def d2d(k, g, half):
        at = pl.ds(half * HR, HR)
        return remote(p0.at[g, at], rb1.at[k, g, at], a_send.at[k, g, half], a_recv.at[k, g, half], sib)

    def ycp(k, g, half):
        at = pl.ds(half * HR, HR)
        return remote(s1.at[g, at], rb2.at[k, g, at], y_send.at[k, g, half], y_recv.at[k, g, half], ypeer)

    def back(k, g, half):
        at = pl.ds(half * HR, HR)
        return remote(t1.at[g, at], rb3.at[k, g, at], b_send.at[k, g, half], b_recv.at[k, g, half], sib)

    def add_core(k, g, half):
        at = slice(half * HR, half * HR + HR)
        d2d(k, g, half).wait_recv()
        s1[g, at] = m0[g, at] + rb1[k, g, at]
        ycp(k, g, half).start()

    def add_chip(k, g, half):
        at = slice(half * HR, half * HR + HR)
        ycp(k, g, half).wait_recv()
        t1[g, at] = s1[g, at] + rb2[k, g, at]
        back(k, g, half).start()

    def settle(k, half, scale_col):
        at = slice(half * HR, half * HR + HR)

        def upd(src, c0):
            to = pl.ds(c0, HC)
            v = src if scale_col is None else scale_col[at] * src
            h[at, to] = (h[at, to] + v).astype(BF16).astype(F32)
        for g in range(NG):
            upd(t1[g, at], half_col(g, core))
        for g in range(NG):
            back(k, g, half).wait_recv()
            upd(rb3[k, g, at], half_col(g, other))

    def drain(k):
        for g in range(NG):
            for half in range(2):
                d2d(k, g, half).wait_send()
                ycp(k, g, half).wait_send()
                back(k, g, half).wait_send()

    def o_products(k, base, half, last):
        at = slice(half * HR, half * HR + HR)
        for g in range(NG):
            i = base + g
            slot = i % NS
            if half == 0:
                wait_item(i)
            r = [big_dot(o2.at[at], lambda k_, w: slots[slot, n * QW + k_:n * QW + k_ + w, :], QW) for n in range(4)]
            p0[g, at] = jnp.concatenate(r[:2], axis=1)
            d2d(k, g, half).start()
            m0[g, at] = jnp.concatenate(r[2:], axis=1)
            if last:
                refill(i, i, i + 1)

    def down_product(base):
        def f(g, part):
            i = base + 4 * g + 2 * part
            r = []
            for n in range(2):
                slot = wait_item(i + n, FF)
                r.append(big_dot(act, lambda k, w: slots[slot, pl.ds(k, w), :], FF))
            for n in range(2):
                refill(i + n, base, base + 16)
            return jnp.concatenate(r, axis=1)
        return f

    def reduce_down(k, base):
        product = down_product(base)

        def body(g, _):
            p0[g] = product(g, 0)
            for half in range(2):
                d2d(k, g, half).start()
            m0[g] = product(g, 1)
            for half in range(2):
                add_core(k, g, half)
            return 0
        lax.fori_loop(0, NG, body, 0)

    def gate_up(base, gain):
        for half in range(2):
            norm_rows(h, gain, x, half * HR, HR)

        def body(j, _):
            i = base + 2 * j
            r = []
            for n in range(2):
                slot = wait_item(i + n)
                r.append(big_dot(x, lambda k, w: slots[slot, pl.ds(k, w), :], W).astype(BF16).astype(F32))
            for n in range(2):
                refill(i + n, base, base + 24)
            gv, uv = r
            act[:, pl.ds(pl.multiple_of(j * QC, QC), QC)] = (gv * (1.0 / (1.0 + jnp.exp(-gv))) * uv).astype(BF16)
            return 0
        lax.fori_loop(0, 12, body, 0)

    rid = iota((R, D), 0)
    maskv = jnp.zeros((R, D), F32)
    for r in range(R):
        maskv = jnp.where(rid == r, mask_s[row0 + r].astype(F32), maskv)
    mask_col = maskv[:, 0:1]

    fin_wait([qcopy])
    for n in range(2 * NG):
        attend_stage(n)
        if n < NG:
            go(kv_self(n + NG))
        else:
            go(kv_cross(n - NG))
    fin_wait([hcopy])
    for c in range(0, W, HC):
        h[:, c:c + HC] = hrow[:, c:c + HC].astype(F32)

    def groups(f, k, half):
        for g in range(NG):
            f(k, g, half)

    base = segs[0][0]
    combine(0)
    o_products(0, base, 0, False)
    groups(add_core, 0, 0)
    combine(1)
    o_products(0, base, 1, True)
    groups(add_chip, 0, 0)
    groups(add_core, 0, 1)
    settle(0, 0, None)
    groups(add_chip, 0, 1)
    settle(0, 1, None)
    drain(0)
    gate_up(segs[1][0], g2)

    reduce_down(1, segs[2][0])
    for half in range(2):
        groups(add_chip, 1, half)
    for half in range(2):
        settle(1, half, None)
    drain(1)

    for half in range(2):
        norm_rows(h, g3, x, half * HR, HR)
    for j in range(NG):
        i = segs[3][0] + j
        slot = wait_item(i)
        y = big_dot(x, lambda k, w: slots[slot, pl.ds(k, w), :], W).astype(BF16).astype(F32)
        refill(i, i, i + 1)
        for hh in range(2):
            t = y[:, hh * D:(hh + 1) * D]
            inv = lax.rsqrt(jnp.mean(t * t, axis=-1, keepdims=True) + NORM_EPS)
            q3[:, 2 * j + hh, :] = (t * inv * qn[...].astype(F32)).astype(BF16).astype(F32)
    fin_wait([xcopy])
    xlen = jnp.sum(jnp.where(xv[...] > 0, 1.0, 0.0), axis=-1, keepdims=True)
    xl[...] = jnp.broadcast_to(2.0 * xlen, (R, D))
    lane2 = iota((HL, 2 * D), 1)
    par2 = (lane2 % 2) == (iota((HL, 2 * D), 0) // 4)
    lanef = lane2.astype(F32)

    for half in range(2):
        fin_wait(kv_cross(2 * half) + kv_cross(2 * half + 1))

        def xbody(it, _):
            res = []
            for u in range(HL):
                v = it * HL + u
                b = half * HR + v
                s = jnp.concatenate([scores(q3[b], kb[2 * half + t, v]) for t in range(2)], axis=1)
                ok = par2 & (lanef < xl[pl.ds(b, 1), :][:, 0:1])
                s = jnp.where(ok, s, NEG_BIG)
                m = jnp.max(s, axis=-1, keepdims=True)
                p = jnp.where(ok, jnp.exp(s - m), 0.0)
                res.append((p, jnp.sum(p, axis=-1, keepdims=True)))
            for u in range(HL):
                v = it * HL + u
                p, l = res[u]
                o = sum(jnp.dot(p[:, t * D:(t + 1) * D].astype(BF16), vb[2 * half + t, v], **WIN) for t in range(2))
                q3[half * HR + v] = o / l
            return 0
        lax.fori_loop(0, HR // HL, xbody, 0)
        flatten(half)

    ga = jnp.tanh(jnp.full((R, 1), gates[0], F32)) * mask_col
    gm2 = jnp.tanh(jnp.full((R, 1), gates[1], F32)) * mask_col
    base = segs[4][0]
    for half in range(2):
        o_products(2, base, half, half == 1)
        groups(add_core, 2, half)
    for half in range(2):
        groups(add_chip, 2, half)
    for half in range(2):
        settle(2, half, ga)
    drain(2)
    gate_up(segs[5][0], g4)

    product = down_product(segs[6][0])

    def quarter(y):
        return pl.ds(pl.multiple_of(y * QC, QC), QC)

    def last_d2d(g):
        return remote(p0.at[g], rb1.at[3, g], a_send.at[3, g, 0], a_recv.at[3, g, 0], sib)

    def qcp(g):
        return remote(s1.at[g, :, quarter(1 - ypos)], rbq.at[g], y_send.at[3, g, 0], y_recv.at[3, g, 0], ypeer)

    def zcp(g, d):
        piece = fin.at[g, core, ypos, sp]
        return remote(piece, piece, z_send.at[g, d], z_recv.at[g, d], {'sp': (sp + d) % NG})

    def fcp(g):
        piece = fin.at[g, core, ypos]
        return remote(piece, piece, f_send.at[g], f_recv.at[g], ypeer)

    def ecp(g):
        piece = fin.at[g, core]
        return remote(piece, piece, e_send.at[g], e_recv.at[g], sib)

    def stage_q(g):
        qcp(g).wait_recv()
        c0 = pl.multiple_of(half_col(g, core) + ypos * QC, QC)
        t = s1[g, :, quarter(ypos)] + rbq[g]
        fin[g, core, ypos, sp] = (h[:, pl.ds(c0, QC)] + gm2 * t).astype(BF16).astype(F32)
        for d in ORDER[:3]:
            zcp(g, d).start()

    def stage_f(g):
        for d in ORDER[:3]:
            zcp(g, d).wait_recv()
        fcp(g).start()

    def stage_e(g):
        fcp(g).wait_recv()
        ecp(g).start()

    def body(g, _):
        p0[g] = product(g, 0)
        last_d2d(g).start()
        mine = product(g, 1)
        last_d2d(g).wait_recv()
        s1[g] = mine + rb1[3, g]
        qcp(g).start()

        @pl.when(g > 0)
        def _():
            stage_q(g - 1)

        @pl.when(g > 1)
        def _():
            stage_f(g - 2)
        return 0
    lax.fori_loop(0, NG, body, 0)
    stage_q(3)
    stage_f(2)
    stage_e(0)
    stage_e(1)
    stage_f(3)
    stage_e(2)
    stage_e(3)

    def emit(g, half):
        for yy in range(2):
            c = pl.multiple_of(half_col(g, half) + yy * QC, QC)
            for zz in range(NG):
                out[zz * R:(zz + 1) * R, pl.ds(c, QC)] = fin[g, half, yy, zz].astype(BF16)
    for g in range(NG):
        emit(g, core)
    for g in range(NG):
        ecp(g).wait_recv()
        emit(g, other)
    for n in range(2 * NG):
        if n % NG < 3:
            sp_copy(n).wait_send()
    for g in range(NG):
        for c in [last_d2d(g), qcp(g), fcp(g), ecp(g)] + [zcp(g, d) for d in ORDER[:3]]:
            c.wait_send()


def solution(mesh):
    cache_spec = P('dp', 'sp', 'tp', None)
    cross_spec = P('dp', None, 'tp', None)
    row_spec = P('dp', None)
    vec_spec = P('dp')
    full_spec = P(None)
    col_spec = P(None, 'tp')
    split_rows = P('tp', None)
    in_specs = (row_spec, vec_spec, cache_spec, cache_spec, cross_spec, cross_spec, row_spec, vec_spec,
                full_spec, col_spec, col_spec, col_spec, split_rows, full_spec, col_spec, col_spec, split_rows,
                full_spec, col_spec, full_spec, split_rows, full_spec, full_spec, col_spec, col_spec, split_rows)
    out_specs = (row_spec, cache_spec, cache_spec)
    vm = pl.BlockSpec(memory_space=VMEM)
    sm = pl.BlockSpec(memory_space=SMEM)
    an = pl.BlockSpec(memory_space=ANY)
    dma = pltpu.SemaphoreType.DMA

    def local_step(hidden, new_pos, k_self, v_self, k_cross, v_cross, xvalid, rowmask,
                   self_attn_norm, self_wq, self_wk, self_wv, self_wo, self_mlp_norm,
                   self_wgate, self_wup, self_wdown, cross_attn_norm, cross_wq, cross_qnorm,
                   cross_wo, cross_gates, cross_mlp_norm, cross_wgate, cross_wup, cross_wdown):
        kc = k_self.reshape(B, D, D)
        vc = v_self.reshape(B, D, D)
        cache = jax.ShapeDtypeStruct((B, D, D), BF16)
        kout, vout, q = pl.pallas_call(
            self_kernel,
            name='self_part',
            out_shape=(cache, cache, jax.ShapeDtypeStruct((B, HL, D), F32)),
            in_specs=[sm, vm] + [an] * 7,
            out_specs=(an, an, an),
            scratch_shapes=[VMEM((B, W), BF16), VMEM((B, W), BF16), VMEM((6, W, QC), BF16),
                            VMEM((B, D, D), BF16), VMEM((B, D, D), BF16),
                            VMEM((B, HL, D), F32), VMEM((2, B, D), F32), VMEM((2, B, D), F32),
                            VMEM((B, D), F32), VMEM((B, D), F32), VMEM((1, D), I32),
                            dma((6,)), dma((8,)), dma((8,)), dma((3,))],
            compiler_params=pltpu.CompilerParams(vmem_limit_bytes=MAXV),
        )(new_pos, self_attn_norm.reshape(R, D), new_pos[None, :], hidden, self_wq, self_wk, self_wv, kc, vc)

        part = VMEM((NG, R, HC), F32)
        parts3 = VMEM((3, NG, R, HC), F32)
        h4 = pl.pallas_call(
            rest_kernel,
            name='rest_part',
            out_shape=jax.ShapeDtypeStruct((B, W), BF16),
            in_specs=[sm, sm, sm, vm, vm, vm, vm] + [an] * 16,
            out_specs=vm,
            scratch_shapes=[
                VMEM((NS, W, QC), BF16), VMEM((B, HL, D), F32), VMEM((NG, 2, HR + 1, HL, D), F32),
                VMEM((NG, 2, HR + 1, HL, D), F32), VMEM((R, W), BF16),
                VMEM((R, W), F32), VMEM((R, W), BF16), VMEM((R, FF), BF16), VMEM((R, QW), BF16),
                VMEM((R, HL, D), F32), VMEM((NG, HR, D, D), BF16), VMEM((NG, HR, D, D), BF16),
                VMEM((R, D), I32), VMEM((R, D), F32),
                part, part, part, part,
                VMEM((4, NG, R, HC), F32), parts3, parts3,
                VMEM((NG, R, QC), F32), VMEM((NG, 2, 2, NG, R, QC), F32),
                dma((NS,)), dma((3,)), dma((2, NG)), dma((2, NG)), dma((2, NG)),
                dma((4, NG, 2)), dma((4, NG, 2)), dma((4, NG, 2)), dma((4, NG, 2)),
                dma((3, NG, 2)), dma((3, NG, 2)), dma((NG, NG)), dma((NG, NG)),
                dma((NG,)), dma((NG,)), dma((NG,)), dma((NG,))],
            compiler_params=pltpu.CompilerParams(collective_id=0, has_side_effects=True,
                                                 vmem_limit_bytes=MAXV),
        )(new_pos, rowmask, cross_gates, self_mlp_norm.reshape(R, D), cross_attn_norm.reshape(R, D),
          cross_mlp_norm.reshape(R, D), cross_qnorm[None, :], q, kout, vout, hidden, xvalid,
          k_cross.reshape(B, 2, D, D), v_cross.reshape(B, 2, D, D),
          self_wo, self_wgate, self_wup, self_wdown, cross_wq, cross_wo, cross_wgate, cross_wup, cross_wdown)
        return h4, kout.reshape(k_self.shape), vout.reshape(v_self.shape)

    return jax.shard_map(local_step, mesh=mesh, in_specs=in_specs, out_specs=out_specs, check_vma=False)
```

time: 420 us -> 146 us (0.35)
  waiting for transfers between devices: 220 us -> 0 us
  Pallas kernels: 0 us -> 143 us
  matrix products: 110 us -> 0 us
  blocking collectives: 42.4 us -> 0 us
  other arithmetic: 29.1 us -> 0 us
  between operations: 14.1 us -> 0.65 us
    psum x5 -> x0, waiting for transfers between devices: 220 us -> none  [the longest x1 51.4 us: local_step(): lax.psum(mlp_partial(rms_norm(after_cross, cross_mlp_norm), cross_wgate,...]
    pallas_call x0 -> x2, Pallas kernels: none -> 143 us  [the longest x1 128 us: local_step(): pl.pallas_call(rest_kernel, name='rest_part', out_shape=jax.ShapeDtypeStr...]
    dot_general x13 -> x0, matrix products: 102 us -> none  [the longest x2 41.2 us: mlp_partial(): return jnp.dot(hidden_act, w_down, preferred_element_type=jnp.float32)]
    pmax x1 -> x0, blocking collectives: 22.9 us -> none  [combine_sp(): glob_max = lax.pmax(part_max, 'sp')]
    psum x1 -> x0, blocking collectives: 19.5 us -> none  [combine_sp(): total_sum = lax.psum(part_sum * factor, 'sp')]
    select_n x2 -> x0, other arithmetic: 12.7 us -> none  [the longest x1 12.7 us: local_step(): k_new_cache = jnp.where(hit_mask, key_new[:, None], k_self)]
    reduce_sum x6 -> x0, other arithmetic: 8.68 us -> none  [the longest x5 7.86 us: rms_norm(): jnp.mean(vals32 * vals32, axis=-1, keepdims=True) + NORM_EPS]
    sub x1 -> x0, matrix products: 8.1 us -> none  [local_softmax(): scores - part_max[..., None]]
  transfers between devices with their start and end apart: 5 -> 0, of which waited for: 5 -> 0; matrix products, arithmetic and copies ran while one was open for 0% -> 0% of each run, Pallas kernels for 0% -> 0%
where the time goes in v1:
time: 146 us; the launch traced here: 145 us
  Pallas kernels  143 us (98%)
  local copies, waits for them, and re-layouts  2.29 us (2%)
    pallas_call x1, Pallas kernels, local_step(): pl.pallas_call(rest_kernel, name='rest_part', out_shape=jax.ShapeDtypeStr...  128 us
    pallas_call x1, Pallas kernels, local_step(): pl.pallas_call(self_kernel, name='self_part', out_shape=(cache, cache, ja...  14.6 us

profile of v1, /device:TPU:0, one launch (start us, length us, event | category | flops | bytes accessed | tf_op | source)
XLA Modules:
  0.0 145.5 jit_solution(16881810061041997007)
XLA Ops:
  0.6 14.6 %self_part.1 = (bf16[128,128,128]{2,1,0:T(8,128)(2,1)}, bf16[128,128,128]{2,1,0:T(8,128)(2,1)}, f32[128,8,128]{2,1,0:T(8,128)}) custom-call(s32[128]{0:T(128)} %pos_s.3, bf16[32,128]{1,0:T(8,128)(2,1)} %bitcast.18, s32[1,128]{1,0:T(1,128)} %bitcast.22, bf16[128,4096]{1,0:T(8,128)(2,1)} %hid.3, bf16[4096,1024]{1,0:T(8,128)(2,1)} %wq.1, bf16[4096,256]{1,0:T(8,128)(2,1)} %wk.1, ...), custom_call_target="tpu_custom_call" | custom-call | tf_op jit(solution)/shard_map/self_part/pallas_call | solution.py:649
  15.2 128.0 %rest_part.1 = bf16[128,4096]{1,0:T(8,128)(2,1)} custom-call(s32[128]{0:T(128)} %pos_s.3, s32[128]{0:T(128)} %mask_s.1, f32[2]{0:T(128)} %gates.1, bf16[32,128]{1,0:T(8,128)(2,1)} %bitcast.19, bf16[32,128]{1,0:T(8,128)(2,1)} %bitcast.20, bf16[32,128]{1,0:T(8,128)(2,1)} %bitcast.21, bf16[1,128]{1,0:T(2,128)(2,1)} %bitcast.23, ...), custom_call_target="tpu_custom_call" | custom-call | tf_op jit(solution)/shard_map/rest_part/pallas_call | solution.py:665
  143.2 2.3 %copy.30 = bf16[128,4096]{1,0:T(8,128)(2,1)} copy(bf16[128,4096]{1,0:T(8,128)(2,1)} %rest_part.1) | data formatting | bytes 2097152

commit v2 on v1

--- a/solution.py
+++ b/solution.py
@@ -20,7 +20,7 @@
 ANY = pl.ANY
 VMEM = pltpu.VMEM
 SMEM = pltpu.SMEM
-NS = 23
+NP = 12
 B = 128
 R = 32
 HR = 16
@@ -159,7 +159,7 @@
 
 def rest_kernel(pos_s, mask_s, gates, g2, g3, g4, qn, q_in, ks, vs, hid, xval, kc, vc,
                 wo, wg1, wu1, wd1, wqc, woc, wg2, wu2, wd2, out,
-                slots, qb, ob, orecv, hrow, h, x, act, o2, q3, kb, vb, xv, xl,
+                slots, qb, ob, orecv, h, x, act, o2, q3, kb, vb, xv, xl,
                 p0, m0, s1, t1, rb1, rb2, rb3, rbq, fin,
                 w_sem, m_sem, k_sem, sp_send, sp_recv, a_send, a_recv, y_send, y_recv,
                 b_send, b_recv, z_send, z_recv, f_send, f_recv, e_send, e_recv):
@@ -182,58 +182,68 @@
         return ref.at[:, pl.ds(pl.multiple_of(c, QC), QC)]
 
     def start(src, dst, slot):
-        pltpu.make_async_copy(src, dst, w_sem.at[slot]).start()
+        pltpu.make_async_copy(src, dst, w_sem.at[slot]).start(priority=1)
 
     def put_o(ref):
         def f(j, slot):
-            for k in range(4):
-                half = other if k < 2 else core
-                start(cols(ref, half_col(j, half) + (k % 2) * QC), slots.at[slot, k * QW:(k + 1) * QW], slot)
+            for n in range(2):
+                for k in range(4):
+                    c = half_col(2 * j + n, other if k < 2 else core) + (k % 2) * QC
+                    start(cols(ref, c), slots.at[slot, n, k * QW:(k + 1) * QW], slot)
         return f
 
     def put_gu(gate, up):
         def f(j, slot):
-            for n, ref in enumerate((gate, up)):
-                @pl.when(j % 2 == n)
-                def _():
-                    start(cols(ref, (j // 2) * QC), slots.at[slot], slot)
+            start(cols(gate, j * QC), slots.at[slot, 0], slot)
+            start(cols(up, j * QC), slots.at[slot, 1], slot)
         return f
 
     def put_down(ref):
         def f(j, slot):
-            k = j % 4
-            half = jnp.where(k < 2, other, core)
-            start(cols(ref, half_col(j // 4, half) + (k % 2) * QC), slots.at[slot, 0:FF], slot)
+            part = j % 2
+            c = half_col(j // 2, other + part * (core - other))
+            for n in range(2):
+                start(cols(ref, c + n * QC), slots.at[slot, n, 0:FF], slot)
         return f
 
     def put_q(ref):
         def f(j, slot):
-            start(cols(ref, j * QC), slots.at[slot], slot)
+            for n in range(2):
+                start(cols(ref, (2 * j + n) * QC), slots.at[slot, n], slot)
         return f
 
-    segs = []
-    pos = 0
-    for count, f in ((4, put_o(wo)), (24, put_gu(wg1, wu1)), (16, put_down(wd1)), (4, put_q(wqc)),
-                     (4, put_o(woc)), (24, put_gu(wg2, wu2)), (16, put_down(wd2))):
-        segs.append((pos, pos + count, f))
-        pos += count
-
-    def issue(i, lo, hi):
-        for a, b, f in segs:
-            if a <= lo and b >= hi:
-                f(i - a, lax.rem(i, NS))
-            elif a < hi and b > lo:
-                @pl.when((i >= a) & (i < b))
-                def _():
-                    f(i - a, lax.rem(i, NS))
-
-    def wait_item(i, depth=W):
-        slot = lax.rem(i, NS)
-        pltpu.make_async_copy(cols(wqc, 0).at[0:depth], slots.at[slot, 0:depth], w_sem.at[slot]).wait()
+    puts = (put_o(wo), put_gu(wg1, wu1), put_down(wd1), put_q(wqc), put_o(woc), put_gu(wg2, wu2), put_down(wd2))
+    starts = [0]
+    for count in (2, 12, 8, 2, 2, 12, 8):
+        starts.append(starts[-1] + count)
+    last_pair = starts.pop()
+
+    def slot_of(seg, j):
+        p = starts[seg] % NP + j
+        if isinstance(p, int):
+            return p % NP
+        return jnp.where(p >= NP, p - NP, p)
+
+    def wait_pair(seg, j, depth=W):
+        slot = slot_of(seg, j)
+        dst = slots.at[slot] if depth == W else slots.at[slot, :, 0:depth]
+        pltpu.make_async_copy(dst, dst, w_sem.at[slot]).wait()
         return slot
 
-    def refill(i, lo, hi):
-        issue(i + NS, lo + NS, hi + NS)
+    def refill(seg, j, first):
+        p = starts[seg] + first + NP
+        if p < last_pair:
+            to = max(n for n in range(len(starts)) if starts[n] <= p)
+            puts[to](j + (starts[seg] + NP - starts[to]), slot_of(seg, j))
+
+    def sub_loops(seg, body):
+        count = {1: 12, 5: 12}[seg]
+        edges = sorted({0, count} | {e - NP - starts[seg] for e in starts + [last_pair] if 0 < e - NP - starts[seg] < count})
+        for a, b in zip(edges, edges[1:]):
+            def run(j, c, a=a):
+                body(j, a)
+                return c
+            lax.fori_loop(a, b, run, 0)
 
     def dest_of(n):
         return (sp + ORDER[n % NG]) % NG
@@ -257,17 +267,20 @@
             c.wait()
 
     qcopy = pltpu.make_async_copy(q_in, qb, m_sem.at[0])
-    hcopy = pltpu.make_async_copy(hid.at[pl.ds(row0, R)], hrow, m_sem.at[1])
+    hcopy = pltpu.make_async_copy(hid.at[pl.ds(row0, R)], x, m_sem.at[1])
     xcopy = pltpu.make_async_copy(xval.at[pl.ds(row0, R)], xv, m_sem.at[2])
     go([qcopy])
     for n in range(NG):
         go(kv_self(n))
     go([hcopy, xcopy])
 
-    def fill(i, _):
-        issue(i, 0, NS)
+    for j in range(2):
+        puts[0](j, slot_of(0, j))
+
+    def fill(j, _):
+        puts[1](j, slot_of(1, j))
         return 0
-    lax.fori_loop(0, NS, fill, 0)
+    lax.fori_loop(0, NP - 2, fill, 0)
 
     barrier = pltpu.get_barrier_semaphore()
     for dev in [{'sp': (sp + d) % NG} for d in ORDER[:3]] + [sib, ypeer]:
@@ -387,61 +400,58 @@
                 ycp(k, g, half).wait_send()
                 back(k, g, half).wait_send()
 
-    def o_products(k, base, half, last):
+    def o_products(k, seg, half, last):
         at = slice(half * HR, half * HR + HR)
         for g in range(NG):
-            i = base + g
-            slot = i % NS
-            if half == 0:
-                wait_item(i)
-            r = [big_dot(o2.at[at], lambda k_, w: slots[slot, n * QW + k_:n * QW + k_ + w, :], QW) for n in range(4)]
+            slot = slot_of(seg, g // 2)
+            if half == 0 and g % 2 == 0:
+                wait_pair(seg, g // 2)
+            r = [jnp.dot(o2[at, :], slots[slot, g % 2, n * QW:(n + 1) * QW, :], **WIN) for n in range(4)]
             p0[g, at] = jnp.concatenate(r[:2], axis=1)
             d2d(k, g, half).start()
             m0[g, at] = jnp.concatenate(r[2:], axis=1)
-            if last:
-                refill(i, i, i + 1)
-
-    def down_product(base):
+            if last and g % 2:
+                refill(seg, g // 2, g // 2)
+
+    def down_product(seg):
         def f(g, part):
-            i = base + 4 * g + 2 * part
-            r = []
-            for n in range(2):
-                slot = wait_item(i + n, FF)
-                r.append(big_dot(act, lambda k, w: slots[slot, pl.ds(k, w), :], FF))
-            for n in range(2):
-                refill(i + n, base, base + 16)
+            j = 2 * g + part
+            slot = wait_pair(seg, j, FF)
+            r = [big_dot(act, lambda k, w: slots[slot, n, pl.ds(k, w), :], FF) for n in range(2)]
+            refill(seg, j, 0)
             return jnp.concatenate(r, axis=1)
         return f
 
-    def reduce_down(k, base):
-        product = down_product(base)
+    def reduce_down(k, seg):
+        product = down_product(seg)
+
+        def both(g):
+            for half in range(2):
+                add_core(k, g, half)
 
         def body(g, _):
             p0[g] = product(g, 0)
             for half in range(2):
                 d2d(k, g, half).start()
+
+            @pl.when(g > 0)
+            def _():
+                both(g - 1)
             m0[g] = product(g, 1)
-            for half in range(2):
-                add_core(k, g, half)
             return 0
         lax.fori_loop(0, NG, body, 0)
-
-    def gate_up(base, gain):
+        both(3)
+
+    def gate_up(seg, gain):
         for half in range(2):
             norm_rows(h, gain, x, half * HR, HR)
 
-        def body(j, _):
-            i = base + 2 * j
-            r = []
-            for n in range(2):
-                slot = wait_item(i + n)
-                r.append(big_dot(x, lambda k, w: slots[slot, pl.ds(k, w), :], W).astype(BF16).astype(F32))
-            for n in range(2):
-                refill(i + n, base, base + 24)
-            gv, uv = r
+        def body(j, first):
+            slot = wait_pair(seg, j)
+            gv, uv = [big_dot(x, lambda k, w: slots[slot, n, pl.ds(k, w), :], W).astype(BF16).astype(F32) for n in range(2)]
+            refill(seg, j, first)
             act[:, pl.ds(pl.multiple_of(j * QC, QC), QC)] = (gv * (1.0 / (1.0 + jnp.exp(-gv))) * uv).astype(BF16)
-            return 0
-        lax.fori_loop(0, 12, body, 0)
+        sub_loops(seg, body)
 
     rid = iota((R, D), 0)
     maskv = jnp.zeros((R, D), F32)
@@ -458,27 +468,26 @@
             go(kv_cross(n - NG))
     fin_wait([hcopy])
     for c in range(0, W, HC):
-        h[:, c:c + HC] = hrow[:, c:c + HC].astype(F32)
+        h[:, c:c + HC] = x[:, c:c + HC].astype(F32)
 
     def groups(f, k, half):
         for g in range(NG):
             f(k, g, half)
 
-    base = segs[0][0]
     combine(0)
-    o_products(0, base, 0, False)
+    o_products(0, 0, 0, False)
     groups(add_core, 0, 0)
     combine(1)
-    o_products(0, base, 1, True)
+    o_products(0, 0, 1, True)
     groups(add_chip, 0, 0)
     groups(add_core, 0, 1)
     settle(0, 0, None)
     groups(add_chip, 0, 1)
     settle(0, 1, None)
     drain(0)
-    gate_up(segs[1][0], g2)
-
-    reduce_down(1, segs[2][0])
+    gate_up(1, g2)
+
+    reduce_down(1, 2)
     for half in range(2):
         groups(add_chip, 1, half)
     for half in range(2):
@@ -487,15 +496,14 @@
 
     for half in range(2):
         norm_rows(h, g3, x, half * HR, HR)
-    for j in range(NG):
-        i = segs[3][0] + j
-        slot = wait_item(i)
-        y = big_dot(x, lambda k, w: slots[slot, pl.ds(k, w), :], W).astype(BF16).astype(F32)
-        refill(i, i, i + 1)
-        for hh in range(2):
-            t = y[:, hh * D:(hh + 1) * D]
+    for j in range(2):
+        slot = wait_pair(3, j)
+        ys = [big_dot(x, lambda k, w: slots[slot, n, pl.ds(k, w), :], W).astype(BF16).astype(F32) for n in range(2)]
+        refill(3, j, j)
+        for hh in range(4):
+            t = ys[hh // 2][:, hh % 2 * D:(hh % 2 + 1) * D]
             inv = lax.rsqrt(jnp.mean(t * t, axis=-1, keepdims=True) + NORM_EPS)
-            q3[:, 2 * j + hh, :] = (t * inv * qn[...].astype(F32)).astype(BF16).astype(F32)
+            q3[:, NG * j + hh, :] = (t * inv * qn[...].astype(F32)).astype(BF16).astype(F32)
     fin_wait([xcopy])
     xlen = jnp.sum(jnp.where(xv[...] > 0, 1.0, 0.0), axis=-1, keepdims=True)
     xl[...] = jnp.broadcast_to(2.0 * xlen, (R, D))
@@ -528,18 +536,17 @@
 
     ga = jnp.tanh(jnp.full((R, 1), gates[0], F32)) * mask_col
     gm2 = jnp.tanh(jnp.full((R, 1), gates[1], F32)) * mask_col
-    base = segs[4][0]
     for half in range(2):
-        o_products(2, base, half, half == 1)
+        o_products(2, 4, half, half == 1)
         groups(add_core, 2, half)
     for half in range(2):
         groups(add_chip, 2, half)
     for half in range(2):
         settle(2, half, ga)
     drain(2)
-    gate_up(segs[5][0], g4)
-
-    product = down_product(segs[6][0])
+    gate_up(5, g4)
+
+    product = down_product(6)
 
     def quarter(y):
         return pl.ds(pl.multiple_of(y * QC, QC), QC)
@@ -579,26 +586,32 @@
         fcp(g).wait_recv()
         ecp(g).start()
 
+    def stage_c(g):
+        last_d2d(g).wait_recv()
+        s1[g] = m0[g] + rb1[3, g]
+        qcp(g).start()
+
     def body(g, _):
         p0[g] = product(g, 0)
         last_d2d(g).start()
-        mine = product(g, 1)
-        last_d2d(g).wait_recv()
-        s1[g] = mine + rb1[3, g]
-        qcp(g).start()
 
         @pl.when(g > 0)
         def _():
-            stage_q(g - 1)
+            stage_c(g - 1)
+        m0[g] = product(g, 1)
 
         @pl.when(g > 1)
         def _():
-            stage_f(g - 2)
+            stage_q(g - 2)
         return 0
     lax.fori_loop(0, NG, body, 0)
+    stage_c(3)
+    stage_q(2)
+    stage_f(0)
     stage_q(3)
+    stage_f(1)
+    stage_e(0)
     stage_f(2)
-    stage_e(0)
     stage_e(1)
     stage_f(3)
     stage_e(2)
@@ -669,15 +682,15 @@
             in_specs=[sm, sm, sm, vm, vm, vm, vm] + [an] * 16,
             out_specs=vm,
             scratch_shapes=[
-                VMEM((NS, W, QC), BF16), VMEM((B, HL, D), F32), VMEM((NG, 2, HR + 1, HL, D), F32),
-                VMEM((NG, 2, HR + 1, HL, D), F32), VMEM((R, W), BF16),
+                VMEM((NP, 2, W, QC), BF16), VMEM((B, HL, D), F32), VMEM((NG, 2, HR + 1, HL, D), F32),
+                VMEM((NG, 2, HR + 1, HL, D), F32),
                 VMEM((R, W), F32), VMEM((R, W), BF16), VMEM((R, FF), BF16), VMEM((R, QW), BF16),
                 VMEM((R, HL, D), F32), VMEM((NG, HR, D, D), BF16), VMEM((NG, HR, D, D), BF16),
                 VMEM((R, D), I32), VMEM((R, D), F32),
                 part, part, part, part,
                 VMEM((4, NG, R, HC), F32), parts3, parts3,
                 VMEM((NG, R, QC), F32), VMEM((NG, 2, 2, NG, R, QC), F32),
-                dma((NS,)), dma((3,)), dma((2, NG)), dma((2, NG)), dma((2, NG)),
+                dma((NP,)), dma((3,)), dma((2, NG)), dma((2, NG)), dma((2, NG)),
                 dma((4, NG, 2)), dma((4, NG, 2)), dma((4, NG, 2)), dma((4, NG, 2)),
                 dma((3, NG, 2)), dma((3, NG, 2)), dma((NG, NG)), dma((NG, NG)),
                 dma((NG,)), dma((NG,)), dma((NG,)), dma((NG,))],

time: 146 us -> 120 us (0.82)
  Pallas kernels: 143 us -> 117 us
    pallas_call x1, Pallas kernels: 128 us -> 103 us  [local_step(): pl.pallas_call(rest_kernel, name='rest_part', out_shape=jax.ShapeDtypeStr...]
where the time goes in v2:
time: 120 us
  Pallas kernels  117 us (98%)
  local copies, waits for them, and re-layouts  2.29 us (2%)
    pallas_call x1, Pallas kernels, local_step(): pl.pallas_call(rest_kernel, name='rest_part', out_shape=jax.ShapeDtypeStr...  103 us
    pallas_call x1, Pallas kernels, local_step(): pl.pallas_call(self_kernel, name='self_part', out_shape=(cache, cache, ja...  14.6 us

profile of v2, /device:TPU:0, one launch (start us, length us, event | category | flops | bytes accessed | tf_op | source)
XLA Modules:
  0.0 120.2 jit_solution(4287207963585207386)
XLA Ops:
  0.6 14.6 %self_part.1 = (bf16[128,128,128]{2,1,0:T(8,128)(2,1)}, bf16[128,128,128]{2,1,0:T(8,128)(2,1)}, f32[128,8,128]{2,1,0:T(8,128)}) custom-call(s32[128]{0:T(128)} %pos_s.3, bf16[32,128]{1,0:T(8,128)(2,1)} %bitcast.18, s32[1,128]{1,0:T(1,128)} %bitcast.22, bf16[128,4096]{1,0:T(8,128)(2,1)} %hid.3, bf16[4096,1024]{1,0:T(8,128)(2,1)} %wq.1, bf16[4096,256]{1,0:T(8,128)(2,1)} %wk.1, ...), custom_call_target="tpu_custom_call" | custom-call | tf_op jit(solution)/shard_map/self_part/pallas_call | solution.py:662
  15.2 102.7 %rest_part.1 = bf16[128,4096]{1,0:T(8,128)(2,1)} custom-call(s32[128]{0:T(128)} %pos_s.3, s32[128]{0:T(128)} %mask_s.1, f32[2]{0:T(128)} %gates.1, bf16[32,128]{1,0:T(8,128)(2,1)} %bitcast.19, bf16[32,128]{1,0:T(8,128)(2,1)} %bitcast.20, bf16[32,128]{1,0:T(8,128)(2,1)} %bitcast.21, bf16[1,128]{1,0:T(2,128)(2,1)} %bitcast.23, ...), custom_call_target="tpu_custom_call" | custom-call | tf_op jit(solution)/shard_map/rest_part/pallas_call | solution.py:678
  117.9 2.3 %copy.30 = bf16[128,4096]{1,0:T(8,128)(2,1)} copy(bf16[128,4096]{1,0:T(8,128)(2,1)} %rest_part.1) | data formatting | bytes 2097152

commit v3 on v2

--- a/solution.py
+++ b/solution.py
@@ -37,7 +37,8 @@
 MAXV = 67043328
 NT = (((1,), (1,)), ((), ()))
 WIN = {'preferred_element_type': F32}
-ORDER = (2, 1, 3, 0)
+ORDER = (2, 3, 1, 0)
+NEAR = (1, 3, 2)
 
 
 def iota(shape, axis):
@@ -97,11 +98,11 @@
     pcopy.start()
     hcopy.start()
     for i in range(2):
-        wcopy(i).start()
-    for j in range(2 * NG):
-        ccopy(j).start()
-    for i in range(2, 6):
-        wcopy(i).start()
+        wcopy(i).start(priority=1)
+    for j in range(NG):
+        wcopy(j + 2).start(priority=1)
+        ccopy(2 * j).start(priority=1)
+        ccopy(2 * j + 1).start(priority=1)
 
     pcopy.wait()
     ri = iota((B, D), 0)
@@ -132,6 +133,7 @@
     project(1)
     row16 = iota((HR, D), 0)
     for j in range(NG):
+        project(j + 2)
         ccopy(2 * j).wait()
         ccopy(2 * j + 1).wait()
 
@@ -149,8 +151,6 @@
         lax.fori_loop(0, R // HL, body, 0)
         ocopy(2 * j).start()
         ocopy(2 * j + 1).start()
-    for i in range(2, 6):
-        project(i)
     qcopy.start()
     for j in range(2 * NG):
         ocopy(j).wait()
@@ -160,7 +160,7 @@
 def rest_kernel(pos_s, mask_s, gates, g2, g3, g4, qn, q_in, ks, vs, hid, xval, kc, vc,
                 wo, wg1, wu1, wd1, wqc, woc, wg2, wu2, wd2, out,
                 slots, qb, ob, orecv, h, x, act, o2, q3, kb, vb, xv, xl,
-                p0, m0, s1, t1, rb1, rb2, rb3, rbq, fin,
+                p0, m0, s1, t1, rb1, rb2, rb3, rbq, fin, ov, v_sem,
                 w_sem, m_sem, k_sem, sp_send, sp_recv, a_send, a_recv, y_send, y_recv,
                 b_send, b_recv, z_send, z_recv, f_send, f_recv, e_send, e_recv):
     sp = lax.axis_index('sp')
@@ -171,6 +171,7 @@
     ypeer = {'tp': (tp + 2) % 4}
     row0 = pl.multiple_of(sp * R, R)
     other = 1 - core
+    turn = jnp.where(sp < 2, 1, -1)
 
     def half_col(g, half):
         return pl.multiple_of(g * 1024 + half * HC, HC)
@@ -246,7 +247,7 @@
             lax.fori_loop(a, b, run, 0)
 
     def dest_of(n):
-        return (sp + ORDER[n % NG]) % NG
+        return (sp + turn * ORDER[n % NG] + NG) % NG
 
     def kv_self(n):
         r = pl.ds(pl.multiple_of(dest_of(n) * R + (n // NG) * HR, HR), HR)
@@ -296,8 +297,12 @@
     def sp_copy(n):
         d = ORDER[n % NG]
         half = n // NG
-        return remote(ob.at[d, half], orecv.at[sp, half], sp_send.at[half, d], sp_recv.at[half, d],
+        return remote(ob.at[d, half], orecv.at[sp, half], sp_send.at[0], sp_recv.at[half, sp],
                       {'sp': dest_of(n)})
+
+    def sp_arrival(half, d):
+        src = (sp + d) % NG
+        return remote(ob.at[d, half], orecv.at[src, half], sp_send.at[0], sp_recv.at[half, src], {'sp': src})
 
     def attend_stage(n):
         half = n // NG
@@ -335,8 +340,8 @@
             orecv[sp, half, HR] = st
 
     def combine(half):
-        for n in range(NG * half, NG * half + 3):
-            sp_copy(n).wait_recv()
+        for d in ORDER[:3]:
+            sp_arrival(half, d).wait_recv()
         st = [orecv[s, half, HR] for s in range(NG)]
         gm = jnp.maximum(jnp.maximum(st[0], st[1]), jnp.maximum(st[2], st[3]))
         fac = [jnp.exp(v - gm) for v in st]
@@ -358,15 +363,15 @@
 
     def d2d(k, g, half):
         at = pl.ds(half * HR, HR)
-        return remote(p0.at[g, at], rb1.at[k, g, at], a_send.at[k, g, half], a_recv.at[k, g, half], sib)
+        return remote(p0.at[g, at], rb1.at[k, g, at], a_send.at[0], a_recv.at[k % 2, g, half], sib)
 
     def ycp(k, g, half):
         at = pl.ds(half * HR, HR)
-        return remote(s1.at[g, at], rb2.at[k, g, at], y_send.at[k, g, half], y_recv.at[k, g, half], ypeer)
+        return remote(s1.at[g, at], rb2.at[k, g, at], y_send.at[0], y_recv.at[k % 2, g, half], ypeer)
 
     def back(k, g, half):
         at = pl.ds(half * HR, HR)
-        return remote(t1.at[g, at], rb3.at[k, g, at], b_send.at[k, g, half], b_recv.at[k, g, half], sib)
+        return remote(t1.at[g, at], rb3.at[k, g, at], b_send.at[0], b_recv.at[k % 2, g, half], sib)
 
     def add_core(k, g, half):
         at = slice(half * HR, half * HR + HR)
@@ -393,12 +398,12 @@
             back(k, g, half).wait_recv()
             upd(rb3[k, g, at], half_col(g, other))
 
+    def sent(ref, sem):
+        pltpu.make_async_copy(ref, ref, sem.at[0]).wait()
+
     def drain(k):
-        for g in range(NG):
-            for half in range(2):
-                d2d(k, g, half).wait_send()
-                ycp(k, g, half).wait_send()
-                back(k, g, half).wait_send()
+        for ref, sem in ((p0, a_send), (s1, y_send), (t1, b_send)):
+            sent(ref, sem)
 
     def o_products(k, seg, half, last):
         at = slice(half * HR, half * HR + HR)
@@ -479,8 +484,8 @@
     groups(add_core, 0, 0)
     combine(1)
     o_products(0, 0, 1, True)
+    groups(add_core, 0, 1)
     groups(add_chip, 0, 0)
-    groups(add_core, 0, 1)
     settle(0, 0, None)
     groups(add_chip, 0, 1)
     settle(0, 1, None)
@@ -552,38 +557,41 @@
         return pl.ds(pl.multiple_of(y * QC, QC), QC)
 
     def last_d2d(g):
-        return remote(p0.at[g], rb1.at[3, g], a_send.at[3, g, 0], a_recv.at[3, g, 0], sib)
+        return remote(p0.at[g], rb1.at[3, g], a_send.at[0], a_recv.at[1, g, 0], sib)
 
     def qcp(g):
-        return remote(s1.at[g, :, quarter(1 - ypos)], rbq.at[g], y_send.at[3, g, 0], y_recv.at[3, g, 0], ypeer)
+        return remote(s1.at[g, :, quarter(1 - ypos)], rbq.at[g], y_send.at[0], y_recv.at[1, g, 0], ypeer)
 
     def zcp(g, d):
         piece = fin.at[g, core, ypos, sp]
-        return remote(piece, piece, z_send.at[g, d], z_recv.at[g, d], {'sp': (sp + d) % NG})
-
-    def fcp(g):
-        piece = fin.at[g, core, ypos]
-        return remote(piece, piece, f_send.at[g], f_recv.at[g], ypeer)
+        return remote(piece, piece, z_send.at[0], z_recv.at[g, d], {'sp': (sp + d) % NG})
+
+    def fcp(g, d):
+        z = (sp + NG - d) % NG
+        piece = fin.at[g, core, ypos, z]
+        return remote(piece, piece, f_send.at[0], f_recv.at[g, d], ypeer)
 
     def ecp(g):
         piece = fin.at[g, core]
-        return remote(piece, piece, e_send.at[g], e_recv.at[g], sib)
+        return remote(piece, piece, e_send.at[0], e_recv.at[g], sib)
 
     def stage_q(g):
         qcp(g).wait_recv()
         c0 = pl.multiple_of(half_col(g, core) + ypos * QC, QC)
         t = s1[g, :, quarter(ypos)] + rbq[g]
         fin[g, core, ypos, sp] = (h[:, pl.ds(c0, QC)] + gm2 * t).astype(BF16).astype(F32)
-        for d in ORDER[:3]:
+        for d in NEAR:
             zcp(g, d).start()
+        fcp(g, 0).start()
 
     def stage_f(g):
-        for d in ORDER[:3]:
+        for d in NEAR:
             zcp(g, d).wait_recv()
-        fcp(g).start()
+            fcp(g, d).start()
 
     def stage_e(g):
-        fcp(g).wait_recv()
+        for d in (0,) + NEAR:
+            fcp(g, d).wait_recv()
         ecp(g).start()
 
     def stage_c(g):
@@ -607,8 +615,8 @@
     lax.fori_loop(0, NG, body, 0)
     stage_c(3)
     stage_q(2)
+    stage_q(3)
     stage_f(0)
-    stage_q(3)
     stage_f(1)
     stage_e(0)
     stage_f(2)
@@ -621,18 +629,26 @@
         for yy in range(2):
             c = pl.multiple_of(half_col(g, half) + yy * QC, QC)
             for zz in range(NG):
-                out[zz * R:(zz + 1) * R, pl.ds(c, QC)] = fin[g, half, yy, zz].astype(BF16)
+                ov[zz * R:(zz + 1) * R, pl.ds(c, QC)] = fin[g, half, yy, zz].astype(BF16)
+
+    def out_copy(g, n):
+        at = pl.ds(half_col(g, (core, other)[n]), HC)
+        return pltpu.make_async_copy(ov.at[:, at], out.at[:, at], v_sem.at[0])
+
     for g in range(NG):
         emit(g, core)
+        out_copy(g, 0).start()
     for g in range(NG):
         ecp(g).wait_recv()
         emit(g, other)
-    for n in range(2 * NG):
-        if n % NG < 3:
-            sp_copy(n).wait_send()
-    for g in range(NG):
-        for c in [last_d2d(g), qcp(g), fcp(g), ecp(g)] + [zcp(g, d) for d in ORDER[:3]]:
-            c.wait_send()
+        out_copy(g, 1).start()
+    pltpu.make_async_copy(ov, out, v_sem.at[0]).wait()
+    sent(ob.at[1:NG], sp_send)
+    sent(p0, a_send)
+    sent(s1.at[:, :, 0:QC], y_send)
+    sent(fin.at[0:3, 0, 0], z_send)
+    sent(fin.at[:, 0, 0], f_send)
+    sent(fin.at[:, 0], e_send)
 
 
 def solution(mesh):
@@ -680,7 +696,7 @@
             name='rest_part',
             out_shape=jax.ShapeDtypeStruct((B, W), BF16),
             in_specs=[sm, sm, sm, vm, vm, vm, vm] + [an] * 16,
-            out_specs=vm,
+            out_specs=an,
             scratch_shapes=[
                 VMEM((NP, 2, W, QC), BF16), VMEM((B, HL, D), F32), VMEM((NG, 2, HR + 1, HL, D), F32),
                 VMEM((NG, 2, HR + 1, HL, D), F32),
@@ -689,11 +705,10 @@
                 VMEM((R, D), I32), VMEM((R, D), F32),
                 part, part, part, part,
                 VMEM((4, NG, R, HC), F32), parts3, parts3,
-                VMEM((NG, R, QC), F32), VMEM((NG, 2, 2, NG, R, QC), F32),
-                dma((NP,)), dma((3,)), dma((2, NG)), dma((2, NG)), dma((2, NG)),
-                dma((4, NG, 2)), dma((4, NG, 2)), dma((4, NG, 2)), dma((4, NG, 2)),
-                dma((3, NG, 2)), dma((3, NG, 2)), dma((NG, NG)), dma((NG, NG)),
-                dma((NG,)), dma((NG,)), dma((NG,)), dma((NG,))],
+                VMEM((NG, R, QC), F32), VMEM((NG, 2, 2, NG, R, QC), F32), VMEM((B, W), BF16), dma((1,)),
+                dma((NP,)), dma((3,)), dma((2, NG)), dma((1,)), dma((2, NG)),
+                dma((1,)), dma((2, NG, 2)), dma((1,)), dma((2, NG, 2)), dma((1,)), dma((2, NG, 2)),
+                dma((1,)), dma((NG, NG)), dma((1,)), dma((NG, NG)), dma((1,)), dma((NG,))],
             compiler_params=pltpu.CompilerParams(collective_id=0, has_side_effects=True,
                                                  vmem_limit_bytes=MAXV),
         )(new_pos, rowmask, cross_gates, self_mlp_norm.reshape(R, D), cross_attn_norm.reshape(R, D),

time: 120 us -> 114 us (0.950)
  Pallas kernels: 117 us -> 111 us
    pallas_call x1, Pallas kernels: 103 us -> 98.4 us  [local_step(): pl.pallas_call(rest_kernel, name='rest_part', out_shape=jax.ShapeDtypeStr...]
    pallas_call x1, Pallas kernels: 14.6 us -> 12.2 us  [local_step(): pl.pallas_call(self_kernel, name='self_part', out_shape=(cache, cache, ja...]
where the time goes in v3:
time: 114 us
  Pallas kernels  111 us (97%)
  local copies, waits for them, and re-layouts  2.29 us (2%)
    pallas_call x1, Pallas kernels, local_step(): pl.pallas_call(rest_kernel, name='rest_part', out_shape=jax.ShapeDtypeStr...  98.4 us
    pallas_call x1, Pallas kernels, local_step(): pl.pallas_call(self_kernel, name='self_part', out_shape=(cache, cache, ja...  12.2 us
    unnamed x1, local copies, waits for them, and re-layouts  2.29 us

profile of v3, /device:TPU:0, one launch (start us, length us, event | category | flops | bytes accessed | tf_op | source)
XLA Modules:
  0.0 113.6 jit_solution(6509335155214398640)
XLA Ops:
  0.6 12.2 %self_part.1 = (bf16[128,128,128]{2,1,0:T(8,128)(2,1)}, bf16[128,128,128]{2,1,0:T(8,128)(2,1)}, f32[128,8,128]{2,1,0:T(8,128)}) custom-call(s32[128]{0:T(128)} %pos_s.3, bf16[32,128]{1,0:T(8,128)(2,1)} %bitcast.18, s32[1,128]{1,0:T(1,128)} %bitcast.22, bf16[128,4096]{1,0:T(8,128)(2,1)} %hid.3, bf16[4096,1024]{1,0:T(8,128)(2,1)} %wq.1, bf16[4096,256]{1,0:T(8,128)(2,1)} %wk.1, ...), custom_call_target="tpu_custom_call" | custom-call | tf_op jit(solution)/shard_map/self_part/pallas_call | solution.py:678
  12.8 98.4 %rest_part.1 = bf16[128,4096]{1,0:T(8,128)(2,1)} custom-call(s32[128]{0:T(128)} %pos_s.3, s32[128]{0:T(128)} %mask_s.1, f32[2]{0:T(128)} %gates.1, bf16[32,128]{1,0:T(8,128)(2,1)} %bitcast.19, bf16[32,128]{1,0:T(8,128)(2,1)} %bitcast.20, bf16[32,128]{1,0:T(8,128)(2,1)} %bitcast.21, bf16[1,128]{1,0:T(2,128)(2,1)} %bitcast.23, ...), custom_call_target="tpu_custom_call" | custom-call | tf_op jit(solution)/shard_map/rest_part/pallas_call | solution.py:694
  111.3 2.3 %copy.30 = bf16[128,4096]{1,0:T(8,128)(2,1)} copy(bf16[128,4096]{1,0:T(8,128)(2,1)} %rest_part.1) | data formatting | bytes 2097152

commit v4 on v3

--- a/solution.py
+++ b/solution.py
@@ -160,7 +160,7 @@
 def rest_kernel(pos_s, mask_s, gates, g2, g3, g4, qn, q_in, ks, vs, hid, xval, kc, vc,
                 wo, wg1, wu1, wd1, wqc, woc, wg2, wu2, wd2, out,
                 slots, qb, ob, orecv, h, x, act, o2, q3, kb, vb, xv, xl,
-                p0, m0, s1, t1, rb1, rb2, rb3, rbq, fin, ov, v_sem,
+                p0, m0, s1, t1, rb1, rb2, rb3, rbq, fin, ov, v_sem, q_sem,
                 w_sem, m_sem, k_sem, sp_send, sp_recv, a_send, a_recv, y_send, y_recv,
                 b_send, b_recv, z_send, z_recv, f_send, f_recv, e_send, e_recv):
     sp = lax.axis_index('sp')
@@ -267,12 +267,15 @@
         for c in cs:
             c.wait()
 
-    qcopy = pltpu.make_async_copy(q_in, qb, m_sem.at[0])
+    def qcopy(n):
+        r = pl.ds(pl.multiple_of(dest_of(n) * R + (n // NG) * HR, HR), HR)
+        return pltpu.make_async_copy(q_in.at[r], qb.at[r], q_sem.at[n])
+
     hcopy = pltpu.make_async_copy(hid.at[pl.ds(row0, R)], x, m_sem.at[1])
     xcopy = pltpu.make_async_copy(xval.at[pl.ds(row0, R)], xv, m_sem.at[2])
-    go([qcopy])
     for n in range(NG):
-        go(kv_self(n))
+        go([qcopy(n)] + kv_self(n))
+    go([qcopy(n) for n in range(NG, 2 * NG)])
     go([hcopy, xcopy])
 
     for j in range(2):
@@ -286,7 +289,6 @@
     barrier = pltpu.get_barrier_semaphore()
     for dev in [{'sp': (sp + d) % NG} for d in ORDER[:3]] + [sib, ypeer]:
         pl.semaphore_signal(barrier, inc=1, device_id=dev, device_id_type=MESH)
-    pl.semaphore_wait(barrier, 5)
 
     lane = iota((HL, D), 1)
     par = (lane % 2) == (iota((HL, D), 0) // 4)
@@ -307,7 +309,7 @@
     def attend_stage(n):
         half = n // NG
         d = ORDER[n % NG]
-        fin_wait(kv_self(n))
+        fin_wait([qcopy(n)] + kv_self(n))
         first = dest_of(n) * R + half * HR
         slot = n % NG
 
@@ -335,6 +337,8 @@
         st = lax.fori_loop(0, HR // HL, body, jnp.zeros((HL, D), F32))
         if d:
             ob[d, half, HR] = st
+            if n == 0:
+                pl.semaphore_wait(barrier, 5)
             sp_copy(n).start()
         else:
             orecv[sp, half, HR] = st
@@ -464,7 +468,6 @@
         maskv = jnp.where(rid == r, mask_s[row0 + r].astype(F32), maskv)
     mask_col = maskv[:, 0:1]
 
-    fin_wait([qcopy])
     for n in range(2 * NG):
         attend_stage(n)
         if n < NG:
@@ -493,8 +496,9 @@
     gate_up(1, g2)
 
     reduce_down(1, 2)
-    for half in range(2):
-        groups(add_chip, 1, half)
+    for g in range(NG):
+        for half in range(2):
+            add_chip(1, g, half)
     for half in range(2):
         settle(1, half, None)
     drain(1)
@@ -538,16 +542,17 @@
             return 0
         lax.fori_loop(0, HR // HL, xbody, 0)
         flatten(half)
+        if half:
+            groups(add_core, 2, 0)
+        o_products(2, 4, half, half == 1)
+    groups(add_core, 2, 1)
 
     ga = jnp.tanh(jnp.full((R, 1), gates[0], F32)) * mask_col
     gm2 = jnp.tanh(jnp.full((R, 1), gates[1], F32)) * mask_col
-    for half in range(2):
-        o_products(2, 4, half, half == 1)
-        groups(add_core, 2, half)
-    for half in range(2):
-        groups(add_chip, 2, half)
-    for half in range(2):
-        settle(2, half, ga)
+    groups(add_chip, 2, 0)
+    settle(2, 0, ga)
+    groups(add_chip, 2, 1)
+    settle(2, 1, ga)
     drain(2)
     gate_up(5, g4)
 
@@ -589,10 +594,22 @@
             zcp(g, d).wait_recv()
             fcp(g, d).start()
 
+    def emit(g, half):
+        for yy in range(2):
+            c = pl.multiple_of(half_col(g, half) + yy * QC, QC)
+            for zz in range(NG):
+                ov[zz * R:(zz + 1) * R, pl.ds(c, QC)] = fin[g, half, yy, zz].astype(BF16)
+
+    def out_copy(g, n):
+        at = pl.ds(half_col(g, (core, other)[n]), HC)
+        return pltpu.make_async_copy(ov.at[:, at], out.at[:, at], v_sem.at[0])
+
     def stage_e(g):
         for d in (0,) + NEAR:
             fcp(g, d).wait_recv()
         ecp(g).start()
+        emit(g, core)
+        out_copy(g, 0).start()
 
     def stage_c(g):
         last_d2d(g).wait_recv()
@@ -625,19 +642,6 @@
     stage_e(2)
     stage_e(3)
 
-    def emit(g, half):
-        for yy in range(2):
-            c = pl.multiple_of(half_col(g, half) + yy * QC, QC)
-            for zz in range(NG):
-                ov[zz * R:(zz + 1) * R, pl.ds(c, QC)] = fin[g, half, yy, zz].astype(BF16)
-
-    def out_copy(g, n):
-        at = pl.ds(half_col(g, (core, other)[n]), HC)
-        return pltpu.make_async_copy(ov.at[:, at], out.at[:, at], v_sem.at[0])
-
-    for g in range(NG):
-        emit(g, core)
-        out_copy(g, 0).start()
     for g in range(NG):
         ecp(g).wait_recv()
         emit(g, other)
@@ -705,7 +709,7 @@
                 VMEM((R, D), I32), VMEM((R, D), F32),
                 part, part, part, part,
                 VMEM((4, NG, R, HC), F32), parts3, parts3,
-                VMEM((NG, R, QC), F32), VMEM((NG, 2, 2, NG, R, QC), F32), VMEM((B, W), BF16), dma((1,)),
+                VMEM((NG, R, QC), F32), VMEM((NG, 2, 2, NG, R, QC), F32), VMEM((B, W), BF16), dma((1,)), dma((2 * NG,)),
                 dma((NP,)), dma((3,)), dma((2, NG)), dma((1,)), dma((2, NG)),
                 dma((1,)), dma((2, NG, 2)), dma((1,)), dma((2, NG, 2)), dma((1,)), dma((2, NG, 2)),
                 dma((1,)), dma((NG, NG)), dma((1,)), dma((NG, NG)), dma((1,)), dma((NG,))],

time: 114 us -> 114 us (level)
  no operation moved by 1% of the time
where the time goes in v4:
time: 114 us; the launch traced here: 113 us
  Pallas kernels  110 us (96%)
  local copies, waits for them, and re-layouts  2.29 us (2%)
    pallas_call x1, Pallas kernels, local_step(): pl.pallas_call(rest_kernel, name='rest_part', out_shape=jax.ShapeDtypeStr...  97.6 us
    pallas_call x1, Pallas kernels, local_step(): pl.pallas_call(self_kernel, name='self_part', out_shape=(cache, cache, ja...  12.2 us
    unnamed x1, local copies, waits for them, and re-layouts  2.29 us

profile of v4, /device:TPU:0, one launch (start us, length us, event | category | flops | bytes accessed | tf_op | source)
XLA Modules:
  0.0 112.7 jit_solution(17962588437105108002)
XLA Ops:
  0.6 12.2 %self_part.1 = (bf16[128,128,128]{2,1,0:T(8,128)(2,1)}, bf16[128,128,128]{2,1,0:T(8,128)(2,1)}, f32[128,8,128]{2,1,0:T(8,128)}) custom-call(s32[128]{0:T(128)} %pos_s.3, bf16[32,128]{1,0:T(8,128)(2,1)} %bitcast.18, s32[1,128]{1,0:T(1,128)} %bitcast.22, bf16[128,4096]{1,0:T(8,128)(2,1)} %hid.3, bf16[4096,1024]{1,0:T(8,128)(2,1)} %wq.1, bf16[4096,256]{1,0:T(8,128)(2,1)} %wk.1, ...), custom_call_target="tpu_custom_call" | custom-call | tf_op jit(solution)/shard_map/self_part/pallas_call | solution.py:682
  12.8 97.6 %rest_part.1 = bf16[128,4096]{1,0:T(8,128)(2,1)} custom-call(s32[128]{0:T(128)} %pos_s.3, s32[128]{0:T(128)} %mask_s.1, f32[2]{0:T(128)} %gates.1, bf16[32,128]{1,0:T(8,128)(2,1)} %bitcast.19, bf16[32,128]{1,0:T(8,128)(2,1)} %bitcast.20, bf16[32,128]{1,0:T(8,128)(2,1)} %bitcast.21, bf16[1,128]{1,0:T(2,128)(2,1)} %bitcast.23, ...), custom_call_target="tpu_custom_call" | custom-call | tf_op jit(solution)/shard_map/rest_part/pallas_call | solution.py:698
  110.4 2.3 %copy.30 = bf16[128,4096]{1,0:T(8,128)(2,1)} copy(bf16[128,4096]{1,0:T(8,128)(2,1)} %rest_part.1) | data formatting | bytes 2097152
